TPU v7x, 1024 devices: a whole 4x4x32 slice. The times are simulated.
1024 devices in a mesh: section: 32 (over z_lo, x), dp: 32 (over y, z_hi, core).
Axes of the slice: x: 4, y: 4, z: 32 (z_hi: 4, z_lo: 8; z = z_hi * 8 + z_lo), core: 2. Of those that a mesh axis runs over, the one named last changes fastest.
Arguments:
- states: bfloat16 [32, 32, 32, 4096], P('dp', 'section'), may hold values from -8 to 8
- memory: bfloat16 [32, 32, 2, 128, 4096], P('dp', 'section'), may hold values from -12 to 12
- memory_len: int32 [32, 32], P('dp', 'section'), may hold values from 2 to 128
- decode_len: int32 [32, 32], P('dp', 'section'), may hold values from 1 to 32
- owner_map: int32 [32], replicated, may hold values from 0 to 31, as said below
- section_gain: bfloat16 [32, 4096], P('section'), may hold values from 0.5 to 2
- cotangent: bfloat16 [32, 3, 32, 32, 4096], P('dp', None, 'section'), may hold values from -18 to 18
Outputs:
- final_states: bfloat16 [32, 32, 32, 4096], P('dp', 'section')
- gain_grad: float32 [32, 4096], P('section')
Inputs may be any that keep to these rules, and one draw needn't show every extreme that they name: owner_map[m] = (m + c) mod 32 for one offset c from 3 to 31, the same for all m.
All inputs are finite; a program needn't handle non-finite values.
Results may differ from a plain program's by a relative error of at most 0.0085.
Values may be sent and summed in bfloat16 or wider, within the bound.
No kernel may reach another device: no remote copies, remote signals or barrier semaphores. Data moves between devices by JAX's collectives and lax.ppermute only.
A program may use at most 32 MiB of HBM per device.

v0:
```python
import jax
import jax.numpy as jnp
from jax import lax
from jax.sharding import PartitionSpec as P

HD = 256
STEPS = 3


def passed_along(value, axis, steps):
    count = lax.axis_size(axis)
    pairs = [(source, (source + steps) % count) for source in range(count)]
    return lax.ppermute(value, axis, pairs)


def attend(queries, key_rows, value_rows, key_live):
    rows_here = queries.shape[0]
    width = queries.shape[1]
    heads_here = width // HD
    query_heads = queries.reshape(rows_here, heads_here, HD)
    key_heads = key_rows.reshape(key_rows.shape[0], heads_here, HD)
    value_heads = value_rows.reshape(value_rows.shape[0], heads_here, HD)
    scores = jnp.einsum(
        "qhd,khd->hqk", query_heads, key_heads, preferred_element_type=jnp.float32
    ) * HD ** (-0.5)
    scores = jnp.where(key_live[None, None, :], scores, jnp.float32(-1e30))
    top = jnp.max(scores, axis=-1, keepdims=True)
    expo = jnp.exp(scores - top)
    probs = (expo / jnp.sum(expo, axis=-1, keepdims=True)).astype(jnp.bfloat16)
    mixed = jnp.einsum("hqk,khd->qhd", probs, value_heads, preferred_element_type=jnp.float32)
    return mixed.reshape(rows_here, width).astype(jnp.bfloat16)


def normalized(state_wide):
    return (
        state_wide * lax.rsqrt(jnp.mean(state_wide * state_wide, axis=-1, keepdims=True) + 1e-06)
    ).astype(jnp.bfloat16)


def per_device(states, memory, memory_len, decode_len, owner_map, section_gain, cotangent):
    sections = lax.axis_size("section")
    levels = (sections - 1).bit_length()
    offset = owner_map[0] % sections
    current = states[0, 0]
    length_wire = decode_len[0, 0].astype(jnp.bfloat16)
    key_rows = memory[0, 0, 0]
    value_rows = memory[0, 0, 1]
    key_live = jnp.arange(key_rows.shape[0]) < memory_len[0, 0]
    gain_total = jnp.zeros((current.shape[1],), jnp.float32)
    row_index = jnp.arange(current.shape[0])[:, None]
    gain_row = section_gain[0].astype(jnp.float32)
    for window_step in range(STEPS):
        distance = (offset - window_step) % sections
        state_wide = current.astype(jnp.float32)
        routed = normalized(state_wide)
        for level in range(levels):
            arrived = passed_along(routed, "section", 2**level)
            routed = jnp.where(distance >> level & 1 == 1, arrived, routed)
        returning = attend(routed, key_rows, value_rows, key_live)
        remaining = (sections - distance) % sections
        for level in range(levels):
            arrived = passed_along(returning, "section", 2**level)
            returning = jnp.where(remaining >> level & 1 == 1, arrived, returning)
        attended = returning.astype(jnp.float32)
        live_rows = row_index < length_wire.astype(jnp.int32)
        cot_now = cotangent[0, window_step, 0].astype(jnp.float32)
        gain_total = gain_total + jnp.sum(
            jnp.where(live_rows, cot_now * attended, jnp.float32(0.0)), axis=0
        )
        current = jnp.where(
            live_rows, state_wide + gain_row[None, :] * attended, state_wide
        ).astype(jnp.bfloat16)
        if window_step + 1 < STEPS:
            current, length_wire = passed_along((current, length_wire), "section", 1)
    summed = lax.psum(gain_total, "dp")
    return (current[None, None], summed[None])


def solution(mesh):
    in_specs = (
        P("dp", "section", None, None),
        P("dp", "section", None, None, None),
        P("dp", "section"),
        P("dp", "section"),
        P(),
        P("section", None),
        P("dp", None, "section", None, None),
    )
    out_specs = (P("dp", "section", None, None), P("section", None))
    return jax.shard_map(
        per_device, mesh=mesh, in_specs=in_specs, out_specs=out_specs, check_vma=False
    )
```

profile of v0, /device:TPU:1, one launch (start us, length us, event | category | flops | bytes accessed | tf_op | source)
XLA Modules:
  0.0 837.9 jit_solution(5931153463526171929)
XLA Ops:
  8.7 13.7 %collective-permute-done.2 = bf16[32,4096]{1,0:T(8,128)(2,1)S(1)} collective-permute-done((bf16[32,4096]{1,0:T(8,128)(2,1)S(1)}, bf16[32,4096]{1,0:T(8,128)(2,1)S(1)}, u32[]{:S(2)}, u32[]{:S(2)}) %collective-permute-start.2) | collective-permute-done | bytes 262176 | tf_op jit(solution)/shard_map/ppermute | solution.py:13
  25.5 14.2 %collective-permute-done.3 = bf16[32,4096]{1,0:T(8,128)(2,1)S(1)} collective-permute-done((bf16[32,4096]{1,0:T(8,128)(2,1)S(1)}, bf16[32,4096]{1,0:T(8,128)(2,1)S(1)}, u32[]{:S(2)}, u32[]{:S(2)}) %collective-permute-start.3) | collective-permute-done | bytes 262176 | tf_op jit(solution)/shard_map/ppermute | solution.py:13
  41.7 12.1 %collective-permute-done.4 = bf16[32,4096]{1,0:T(8,128)(2,1)S(1)} collective-permute-done((bf16[32,4096]{1,0:T(8,128)(2,1)S(1)}, bf16[32,4096]{1,0:T(8,128)(2,1)S(1)}, u32[]{:S(2)}, u32[]{:S(2)}) %collective-permute-start.4) | collective-permute-done | bytes 262176 | tf_op jit(solution)/shard_map/ppermute | solution.py:13
  55.7 16.6 %collective-permute-done.5 = bf16[32,4096]{1,0:T(8,128)(2,1)S(1)} collective-permute-done((bf16[32,4096]{1,0:T(8,128)(2,1)S(1)}, bf16[32,4096]{1,0:T(8,128)(2,1)S(1)}, u32[]{:S(2)}, u32[]{:S(2)}) %collective-permute-start.5) | collective-permute-done | bytes 262176 | tf_op jit(solution)/shard_map/ppermute | solution.py:13
  78.0 16.8 %collective-permute-done.6 = bf16[32,4096]{1,0:T(8,128)(2,1)} collective-permute-done((bf16[32,4096]{1,0:T(8,128)(2,1)S(1)}, bf16[32,4096]{1,0:T(8,128)(2,1)}, u32[]{:S(2)}, u32[]{:S(2)}) %collective-permute-start.6) | collective-permute-done | bytes 262176 | tf_op jit(solution)/shard_map/ppermute | solution.py:13
  99.4 13.9 %collective-permute-done.7 = bf16[32,4096]{1,0:T(8,128)(2,1)S(1)} collective-permute-done((bf16[32,4096]{1,0:T(8,128)(2,1)S(1)}, bf16[32,4096]{1,0:T(8,128)(2,1)S(1)}, u32[]{:S(2)}, u32[]{:S(2)}) %collective-permute-start.7) | collective-permute-done | bytes 262176 | tf_op jit(solution)/shard_map/ppermute | solution.py:13
  115.2 14.2 %collective-permute-done.8 = bf16[32,4096]{1,0:T(8,128)(2,1)S(1)} collective-permute-done((bf16[32,4096]{1,0:T(8,128)(2,1)S(1)}, bf16[32,4096]{1,0:T(8,128)(2,1)S(1)}, u32[]{:S(2)}, u32[]{:S(2)}) %collective-permute-start.8) | collective-permute-done | bytes 262176 | tf_op jit(solution)/shard_map/ppermute | solution.py:13
  131.4 11.8 %collective-permute-done.9 = bf16[32,4096]{1,0:T(8,128)(2,1)S(1)} collective-permute-done((bf16[32,4096]{1,0:T(8,128)(2,1)S(1)}, bf16[32,4096]{1,0:T(8,128)(2,1)S(1)}, u32[]{:S(2)}, u32[]{:S(2)}) %collective-permute-start.9) | collective-permute-done | bytes 262176 | tf_op jit(solution)/shard_map/ppermute | solution.py:13
  145.1 16.6 %collective-permute-done.10 = bf16[32,4096]{1,0:T(8,128)(2,1)S(1)} collective-permute-done((bf16[32,4096]{1,0:T(8,128)(2,1)S(1)}, bf16[32,4096]{1,0:T(8,128)(2,1)S(1)}, u32[]{:S(2)}, u32[]{:S(2)}) %collective-permute-start.10) | collective-permute-done | bytes 262176 | tf_op jit(solution)/shard_map/ppermute | solution.py:13
  164.4 19.7 %collective-permute-done.11 = bf16[32,4096]{1,0:T(8,128)(2,1)S(1)} collective-permute-done((bf16[32,4096]{1,0:T(8,128)(2,1)S(1)}, bf16[32,4096]{1,0:T(8,128)(2,1)S(1)}, u32[]{:S(2)}, u32[]{:S(2)}) %collective-permute-start.11) | collective-permute-done | bytes 262176 | tf_op jit(solution)/shard_map/ppermute | solution.py:13
  186.2 13.9 %collective-permute-done.12 = bf16[32,4096]{1,0:T(8,128)(2,1)S(1)} collective-permute-done((bf16[32,4096]{1,0:T(8,128)(2,1)S(1)}, bf16[32,4096]{1,0:T(8,128)(2,1)S(1)}, u32[]{:S(2)}, u32[]{:S(2)}) %collective-permute-start.12) | collective-permute-done | bytes 262176 | tf_op jit(solution)/shard_map/ppermute | solution.py:13
  202.4 13.9 %collective-permute-done.13 = bf16[32,4096]{1,0:T(8,128)(2,1)S(1)} collective-permute-done((bf16[32,4096]{1,0:T(8,128)(2,1)S(1)}, bf16[32,4096]{1,0:T(8,128)(2,1)S(1)}, u32[]{:S(2)}, u32[]{:S(2)}) %collective-permute-start.13) | collective-permute-done | bytes 262176 | tf_op jit(solution)/shard_map/ppermute | solution.py:13
  218.4 14.3 %collective-permute-done.14 = bf16[32,4096]{1,0:T(8,128)(2,1)} collective-permute-done((bf16[32,4096]{1,0:T(8,128)(2,1)S(1)}, bf16[32,4096]{1,0:T(8,128)(2,1)}, u32[]{:S(2)}, u32[]{:S(2)}) %collective-permute-start.14) | collective-permute-done | bytes 262176 | tf_op jit(solution)/shard_map/ppermute | solution.py:13
  234.6 11.9 %collective-permute-done.15 = bf16[32,4096]{1,0:T(8,128)(2,1)} collective-permute-done((bf16[32,4096]{1,0:T(8,128)(2,1)S(1)}, bf16[32,4096]{1,0:T(8,128)(2,1)}, u32[]{:S(2)}, u32[]{:S(2)}) %collective-permute-start.15) | collective-permute-done | bytes 262176 | tf_op jit(solution)/shard_map/ppermute | solution.py:13
  249.4 16.7 %collective-permute-done.16 = bf16[32,4096]{1,0:T(8,128)(2,1)} collective-permute-done((bf16[32,4096]{1,0:T(8,128)(2,1)S(1)}, bf16[32,4096]{1,0:T(8,128)(2,1)}, u32[]{:S(2)}, u32[]{:S(2)}) %collective-permute-start.16) | collective-permute-done | bytes 262176 | tf_op jit(solution)/shard_map/ppermute | solution.py:13
  268.1 17.5 %collective-permute-done.17 = bf16[32,4096]{1,0:T(8,128)(2,1)S(1)} collective-permute-done((bf16[32,4096]{1,0:T(8,128)(2,1)S(1)}, bf16[32,4096]{1,0:T(8,128)(2,1)S(1)}, u32[]{:S(2)}, u32[]{:S(2)}) %collective-permute-start.17) | collective-permute-done | bytes 262176 | tf_op jit(solution)/shard_map/ppermute | solution.py:13
  289.1 14.0 %collective-permute-done.18 = bf16[32,4096]{1,0:T(8,128)(2,1)} collective-permute-done((bf16[32,4096]{1,0:T(8,128)(2,1)S(1)}, bf16[32,4096]{1,0:T(8,128)(2,1)}, u32[]{:S(2)}, u32[]{:S(2)}) %collective-permute-start.18) | collective-permute-done | bytes 262176 | tf_op jit(solution)/shard_map/ppermute | solution.py:13
  306.0 14.3 %collective-permute-done.19 = bf16[32,4096]{1,0:T(8,128)(2,1)} collective-permute-done((bf16[32,4096]{1,0:T(8,128)(2,1)S(1)}, bf16[32,4096]{1,0:T(8,128)(2,1)}, u32[]{:S(2)}, u32[]{:S(2)}) %collective-permute-start.19) | collective-permute-done | bytes 262176 | tf_op jit(solution)/shard_map/ppermute | solution.py:13
  323.2 11.9 %collective-permute-done.20 = bf16[32,4096]{1,0:T(8,128)(2,1)} collective-permute-done((bf16[32,4096]{1,0:T(8,128)(2,1)S(1)}, bf16[32,4096]{1,0:T(8,128)(2,1)}, u32[]{:S(2)}, u32[]{:S(2)}) %collective-permute-start.20) | collective-permute-done | bytes 262176 | tf_op jit(solution)/shard_map/ppermute | solution.py:13
  337.1 16.7 %collective-permute-done.21 = bf16[32,4096]{1,0:T(8,128)(2,1)} collective-permute-done((bf16[32,4096]{1,0:T(8,128)(2,1)S(1)}, bf16[32,4096]{1,0:T(8,128)(2,1)}, u32[]{:S(2)}, u32[]{:S(2)}) %collective-permute-start.21) | collective-permute-done | bytes 262176 | tf_op jit(solution)/shard_map/ppermute | solution.py:13
  376.1 13.9 %collective-permute-done.23 = bf16[32,4096]{1,0:T(8,128)(2,1)S(1)} collective-permute-done((bf16[32,4096]{1,0:T(8,128)(2,1)S(1)}, bf16[32,4096]{1,0:T(8,128)(2,1)S(1)}, u32[]{:S(2)}, u32[]{:S(2)}) %collective-permute-start.23) | collective-permute-done | bytes 262176 | tf_op jit(solution)/shard_map/ppermute | solution.py:13
  393.0 14.2 %collective-permute-done.24 = bf16[32,4096]{1,0:T(8,128)(2,1)} collective-permute-done((bf16[32,4096]{1,0:T(8,128)(2,1)}, bf16[32,4096]{1,0:T(8,128)(2,1)}, u32[]{:S(2)}, u32[]{:S(2)}) %collective-permute-start.24) | collective-permute-done | bytes 262176 | tf_op jit(solution)/shard_map/ppermute | solution.py:13
  409.9 14.5 %collective-permute-done.25 = bf16[32,4096]{1,0:T(8,128)(2,1)} collective-permute-done((bf16[32,4096]{1,0:T(8,128)(2,1)}, bf16[32,4096]{1,0:T(8,128)(2,1)}, u32[]{:S(2)}, u32[]{:S(2)}) %collective-permute-start.25) | collective-permute-done | bytes 262176 | tf_op jit(solution)/shard_map/ppermute | solution.py:13
  428.0 12.1 %collective-permute-done.26 = bf16[32,4096]{1,0:T(8,128)(2,1)} collective-permute-done((bf16[32,4096]{1,0:T(8,128)(2,1)}, bf16[32,4096]{1,0:T(8,128)(2,1)}, u32[]{:S(2)}, u32[]{:S(2)}) %collective-permute-start.26) | collective-permute-done | bytes 262176 | tf_op jit(solution)/shard_map/ppermute | solution.py:13
  443.8 15.2 %collective-permute-done.27 = bf16[32,4096]{1,0:T(8,128)(2,1)} collective-permute-done((bf16[32,4096]{1,0:T(8,128)(2,1)}, bf16[32,4096]{1,0:T(8,128)(2,1)}, u32[]{:S(2)}, u32[]{:S(2)}) %collective-permute-start.27) | collective-permute-done | bytes 262176 | tf_op jit(solution)/shard_map/ppermute | solution.py:13
  462.5 19.7 %collective-permute-done.28 = bf16[32,4096]{1,0:T(8,128)(2,1)} collective-permute-done((bf16[32,4096]{1,0:T(8,128)(2,1)}, bf16[32,4096]{1,0:T(8,128)(2,1)}, u32[]{:S(2)}, u32[]{:S(2)}) %collective-permute-start.28) | collective-permute-done | bytes 262176 | tf_op jit(solution)/shard_map/ppermute | solution.py:13
  489.6 13.9 %collective-permute-done.29 = bf16[32,4096]{1,0:T(8,128)(2,1)S(1)} collective-permute-done((bf16[32,4096]{1,0:T(8,128)(2,1)S(1)}, bf16[32,4096]{1,0:T(8,128)(2,1)S(1)}, u32[]{:S(2)}, u32[]{:S(2)}) %collective-permute-start.29) | collective-permute-done | bytes 262176 | tf_op jit(solution)/shard_map/ppermute | solution.py:13
  505.4 14.2 %collective-permute-done.30 = bf16[32,4096]{1,0:T(8,128)(2,1)S(1)} collective-permute-done((bf16[32,4096]{1,0:T(8,128)(2,1)S(1)}, bf16[32,4096]{1,0:T(8,128)(2,1)S(1)}, u32[]{:S(2)}, u32[]{:S(2)}) %collective-permute-start.30) | collective-permute-done | bytes 262176 | tf_op jit(solution)/shard_map/ppermute | solution.py:13
  521.6 11.8 %collective-permute-done.31 = bf16[32,4096]{1,0:T(8,128)(2,1)S(1)} collective-permute-done((bf16[32,4096]{1,0:T(8,128)(2,1)S(1)}, bf16[32,4096]{1,0:T(8,128)(2,1)S(1)}, u32[]{:S(2)}, u32[]{:S(2)}) %collective-permute-start.31) | collective-permute-done | bytes 262176 | tf_op jit(solution)/shard_map/ppermute | solution.py:13
  535.3 16.6 %collective-permute-done.32 = bf16[32,4096]{1,0:T(8,128)(2,1)S(1)} collective-permute-done((bf16[32,4096]{1,0:T(8,128)(2,1)S(1)}, bf16[32,4096]{1,0:T(8,128)(2,1)S(1)}, u32[]{:S(2)}, u32[]{:S(2)}) %collective-permute-start.32) | collective-permute-done | bytes 262176 | tf_op jit(solution)/shard_map/ppermute | solution.py:13
  555.8 11.4 %collective-permute-done.1 = bf16[]{:T(256)} collective-permute-done((bf16[]{:T(256)}, bf16[]{:T(256)}, u32[]{:S(2)}, u32[]{:S(2)}) %collective-permute-start.1) | collective-permute-done | bytes 34 | tf_op jit(solution)/shard_map/ppermute | solution.py:13
  574.0 263.9 %psum.7 = f32[1,4096]{1,0:T(1,128)} all-reduce(f32[1,4096]{1,0:T(1,128)S(1)} %bitcast.81), channel_id=1, replica_groups=mesh['section'=32,'dp'=32] {'dp'}, use_global_device_ids=true, to_apply=%region_12.13 | all-reduce | flops 4096 | bytes 32768 | tf_op jit(solution)/shard_map/psum | solution.py:75
  (103 shorter events, 115.9 us)
Async XLA Ops:
  2.8 19.7 %collective-permute-start.2 = (bf16[32,4096]{1,0:T(8,128)(2,1)S(1)}, bf16[32,4096]{1,0:T(8,128)(2,1)S(1)}, u32[]{:S(2)}, u32[]{:S(2)}) collective-permute-start(bf16[32,4096]{1,0:T(8,128)(2,1)S(1)} %fusion.28), channel_id=1, source_target_pairs={{0,32},{32,64},{64,96},{96,128},{128,160},{160,192},{192,224},{224... | collective-permute-start | bytes 786440 | tf_op jit(solution)/shard_map/ppermute | solution.py:13
  23.6 16.1 %collective-permute-start.3 = (bf16[32,4096]{1,0:T(8,128)(2,1)S(1)}, bf16[32,4096]{1,0:T(8,128)(2,1)S(1)}, u32[]{:S(2)}, u32[]{:S(2)}) collective-permute-start(bf16[32,4096]{1,0:T(8,128)(2,1)S(1)} %broadcast_select_fusion.20), channel_id=1, source_target_pairs={{0,64},{32,96},{64,128},{96,160},{128,192},{160,224},{192,256},{22... | collective-permute-start | bytes 786440 | tf_op jit(solution)/shard_map/ppermute | solution.py:13
  39.7 14.0 %collective-permute-start.4 = (bf16[32,4096]{1,0:T(8,128)(2,1)S(1)}, bf16[32,4096]{1,0:T(8,128)(2,1)S(1)}, u32[]{:S(2)}, u32[]{:S(2)}) collective-permute-start(bf16[32,4096]{1,0:T(8,128)(2,1)S(1)} %broadcast_select_fusion.21), channel_id=1, source_target_pairs={{0,128},{32,160},{64,192},{96,224},{128,256},{160,288},{192,320},{... | collective-permute-start | bytes 786440 | tf_op jit(solution)/shard_map/ppermute | solution.py:13
  53.8 18.5 %collective-permute-start.5 = (bf16[32,4096]{1,0:T(8,128)(2,1)S(1)}, bf16[32,4096]{1,0:T(8,128)(2,1)S(1)}, u32[]{:S(2)}, u32[]{:S(2)}) collective-permute-start(bf16[32,4096]{1,0:T(8,128)(2,1)S(1)} %broadcast_select_fusion.22), channel_id=1, source_target_pairs={{0,256},{32,288},{64,320},{96,352},{128,384},{160,416},{192,448},{... | collective-permute-start | bytes 786440 | tf_op jit(solution)/shard_map/ppermute | solution.py:13
  72.4 22.4 %collective-permute-start.6 = (bf16[32,4096]{1,0:T(8,128)(2,1)S(1)}, bf16[32,4096]{1,0:T(8,128)(2,1)}, u32[]{:S(2)}, u32[]{:S(2)}) collective-permute-start(bf16[32,4096]{1,0:T(8,128)(2,1)S(1)} %broadcast_select_fusion.23), channel_id=1, source_target_pairs={{0,512},{32,544},{64,576},{96,608},{128,640},{160,672},{192,704},{... | collective-permute-start | bytes 786440 | tf_op jit(solution)/shard_map/ppermute | solution.py:13
  97.3 16.0 %collective-permute-start.7 = (bf16[32,4096]{1,0:T(8,128)(2,1)S(1)}, bf16[32,4096]{1,0:T(8,128)(2,1)S(1)}, u32[]{:S(2)}, u32[]{:S(2)}) collective-permute-start(bf16[32,4096]{1,0:T(8,128)(2,1)S(1)} %bitcast.71), channel_id=1, source_target_pairs={{0,32},{32,64},{64,96},{96,128},{128,160},{160,192},{192,224},{224... | collective-permute-start | bytes 786440 | tf_op jit(solution)/shard_map/ppermute | solution.py:13
  113.3 16.1 %collective-permute-start.8 = (bf16[32,4096]{1,0:T(8,128)(2,1)S(1)}, bf16[32,4096]{1,0:T(8,128)(2,1)S(1)}, u32[]{:S(2)}, u32[]{:S(2)}) collective-permute-start(bf16[32,4096]{1,0:T(8,128)(2,1)S(1)} %broadcast_select_fusion.25), channel_id=1, source_target_pairs={{0,64},{32,96},{64,128},{96,160},{128,192},{160,224},{192,256},{22... | collective-permute-start | bytes 786440 | tf_op jit(solution)/shard_map/ppermute | solution.py:13
  129.5 13.7 %collective-permute-start.9 = (bf16[32,4096]{1,0:T(8,128)(2,1)S(1)}, bf16[32,4096]{1,0:T(8,128)(2,1)S(1)}, u32[]{:S(2)}, u32[]{:S(2)}) collective-permute-start(bf16[32,4096]{1,0:T(8,128)(2,1)S(1)} %broadcast_select_fusion.26), channel_id=1, source_target_pairs={{0,128},{32,160},{64,192},{96,224},{128,256},{160,288},{192,320},{... | collective-permute-start | bytes 786440 | tf_op jit(solution)/shard_map/ppermute | solution.py:13
  143.2 18.5 %collective-permute-start.10 = (bf16[32,4096]{1,0:T(8,128)(2,1)S(1)}, bf16[32,4096]{1,0:T(8,128)(2,1)S(1)}, u32[]{:S(2)}, u32[]{:S(2)}) collective-permute-start(bf16[32,4096]{1,0:T(8,128)(2,1)S(1)} %broadcast_select_fusion.27), channel_id=1, source_target_pairs={{0,256},{32,288},{64,320},{96,352},{128,384},{160,416},{192,448},{... | collective-permute-start | bytes 786440 | tf_op jit(solution)/shard_map/ppermute | solution.py:13
  161.8 22.3 %collective-permute-start.11 = (bf16[32,4096]{1,0:T(8,128)(2,1)S(1)}, bf16[32,4096]{1,0:T(8,128)(2,1)S(1)}, u32[]{:S(2)}, u32[]{:S(2)}) collective-permute-start(bf16[32,4096]{1,0:T(8,128)(2,1)S(1)} %broadcast_select_fusion.28), channel_id=1, source_target_pairs={{0,512},{32,544},{64,576},{96,608},{128,640},{160,672},{192,704},{... | collective-permute-start | bytes 786440 | tf_op jit(solution)/shard_map/ppermute | solution.py:13
  184.3 15.8 %collective-permute-start.12 = (bf16[32,4096]{1,0:T(8,128)(2,1)S(1)}, bf16[32,4096]{1,0:T(8,128)(2,1)S(1)}, u32[]{:S(2)}, u32[]{:S(2)}) collective-permute-start(bf16[32,4096]{1,0:T(8,128)(2,1)S(1)} %fusion.29), channel_id=1, source_target_pairs={{0,32},{32,64},{64,96},{96,128},{128,160},{160,192},{192,224},{224... | collective-permute-start | bytes 786440 | tf_op jit(solution)/shard_map/ppermute | solution.py:13
  200.4 15.8 %collective-permute-start.13 = (bf16[32,4096]{1,0:T(8,128)(2,1)S(1)}, bf16[32,4096]{1,0:T(8,128)(2,1)S(1)}, u32[]{:S(2)}, u32[]{:S(2)}) collective-permute-start(bf16[32,4096]{1,0:T(8,128)(2,1)S(1)} %fusion.22), channel_id=1, source_target_pairs={{0,32},{32,64},{64,96},{96,128},{128,160},{160,192},{192,224},{224... | collective-permute-start | bytes 786440 | tf_op jit(solution)/shard_map/ppermute | solution.py:13
  216.4 16.2 %collective-permute-start.14 = (bf16[32,4096]{1,0:T(8,128)(2,1)S(1)}, bf16[32,4096]{1,0:T(8,128)(2,1)}, u32[]{:S(2)}, u32[]{:S(2)}) collective-permute-start(bf16[32,4096]{1,0:T(8,128)(2,1)S(1)} %broadcast_select_fusion.10), channel_id=1, source_target_pairs={{0,64},{32,96},{64,128},{96,160},{128,192},{160,224},{192,256},{22... | collective-permute-start | bytes 786440 | tf_op jit(solution)/shard_map/ppermute | solution.py:13
  232.7 13.8 %collective-permute-start.15 = (bf16[32,4096]{1,0:T(8,128)(2,1)S(1)}, bf16[32,4096]{1,0:T(8,128)(2,1)}, u32[]{:S(2)}, u32[]{:S(2)}) collective-permute-start(bf16[32,4096]{1,0:T(8,128)(2,1)S(1)} %broadcast_select_fusion.11), channel_id=1, source_target_pairs={{0,128},{32,160},{64,192},{96,224},{128,256},{160,288},{192,320},{... | collective-permute-start | bytes 786440 | tf_op jit(solution)/shard_map/ppermute | solution.py:13
  247.5 18.6 %collective-permute-start.16 = (bf16[32,4096]{1,0:T(8,128)(2,1)S(1)}, bf16[32,4096]{1,0:T(8,128)(2,1)}, u32[]{:S(2)}, u32[]{:S(2)}) collective-permute-start(bf16[32,4096]{1,0:T(8,128)(2,1)S(1)} %broadcast_select_fusion.12), channel_id=1, source_target_pairs={{0,256},{32,288},{64,320},{96,352},{128,384},{160,416},{192,448},{... | collective-permute-start | bytes 786440 | tf_op jit(solution)/shard_map/ppermute | solution.py:13
  266.2 19.4 %collective-permute-start.17 = (bf16[32,4096]{1,0:T(8,128)(2,1)S(1)}, bf16[32,4096]{1,0:T(8,128)(2,1)S(1)}, u32[]{:S(2)}, u32[]{:S(2)}) collective-permute-start(bf16[32,4096]{1,0:T(8,128)(2,1)S(1)} %broadcast_select_fusion.13), channel_id=1, source_target_pairs={{0,512},{32,544},{64,576},{96,608},{128,640},{160,672},{192,704},{... | collective-permute-start | bytes 786440 | tf_op jit(solution)/shard_map/ppermute | solution.py:13
  287.1 15.9 %collective-permute-start.18 = (bf16[32,4096]{1,0:T(8,128)(2,1)S(1)}, bf16[32,4096]{1,0:T(8,128)(2,1)}, u32[]{:S(2)}, u32[]{:S(2)}) collective-permute-start(bf16[32,4096]{1,0:T(8,128)(2,1)S(1)} %bitcast.73), channel_id=1, source_target_pairs={{0,32},{32,64},{64,96},{96,128},{128,160},{160,192},{192,224},{224... | collective-permute-start | bytes 786440 | tf_op jit(solution)/shard_map/ppermute | solution.py:13
  304.1 16.2 %collective-permute-start.19 = (bf16[32,4096]{1,0:T(8,128)(2,1)S(1)}, bf16[32,4096]{1,0:T(8,128)(2,1)}, u32[]{:S(2)}, u32[]{:S(2)}) collective-permute-start(bf16[32,4096]{1,0:T(8,128)(2,1)S(1)} %broadcast_select_fusion.15), channel_id=1, source_target_pairs={{0,64},{32,96},{64,128},{96,160},{128,192},{160,224},{192,256},{22... | collective-permute-start | bytes 786440 | tf_op jit(solution)/shard_map/ppermute | solution.py:13
  321.3 13.8 %collective-permute-start.20 = (bf16[32,4096]{1,0:T(8,128)(2,1)S(1)}, bf16[32,4096]{1,0:T(8,128)(2,1)}, u32[]{:S(2)}, u32[]{:S(2)}) collective-permute-start(bf16[32,4096]{1,0:T(8,128)(2,1)S(1)} %broadcast_select_fusion.16), channel_id=1, source_target_pairs={{0,128},{32,160},{64,192},{96,224},{128,256},{160,288},{192,320},{... | collective-permute-start | bytes 786440 | tf_op jit(solution)/shard_map/ppermute | solution.py:13
  335.1 18.6 %collective-permute-start.21 = (bf16[32,4096]{1,0:T(8,128)(2,1)S(1)}, bf16[32,4096]{1,0:T(8,128)(2,1)}, u32[]{:S(2)}, u32[]{:S(2)}) collective-permute-start(bf16[32,4096]{1,0:T(8,128)(2,1)S(1)} %broadcast_select_fusion.17), channel_id=1, source_target_pairs={{0,256},{32,288},{64,320},{96,352},{128,384},{160,416},{192,448},{... | collective-permute-start | bytes 786440 | tf_op jit(solution)/shard_map/ppermute | solution.py:13
  354.8 19.3 %collective-permute-start.22 = (bf16[32,4096]{1,0:T(8,128)(2,1)S(1)}, bf16[32,4096]{1,0:T(8,128)(2,1)S(1)}, u32[]{:S(2)}, u32[]{:S(2)}) collective-permute-start(bf16[32,4096]{1,0:T(8,128)(2,1)S(1)} %broadcast_select_fusion.18), channel_id=1, source_target_pairs={{0,512},{32,544},{64,576},{96,608},{128,640},{160,672},{192,704},{... | collective-permute-start | bytes 786440 | tf_op jit(solution)/shard_map/ppermute | solution.py:13
  374.2 15.8 %collective-permute-start.23 = (bf16[32,4096]{1,0:T(8,128)(2,1)S(1)}, bf16[32,4096]{1,0:T(8,128)(2,1)S(1)}, u32[]{:S(2)}, u32[]{:S(2)}) collective-permute-start(bf16[32,4096]{1,0:T(8,128)(2,1)S(1)} %fusion.23), channel_id=1, source_target_pairs={{0,32},{32,64},{64,96},{96,128},{128,160},{160,192},{192,224},{224... | collective-permute-start | bytes 786440 | tf_op jit(solution)/shard_map/ppermute | solution.py:13
  391.0 16.1 %collective-permute-start.24 = (bf16[32,4096]{1,0:T(8,128)(2,1)}, bf16[32,4096]{1,0:T(8,128)(2,1)}, u32[]{:S(2)}, u32[]{:S(2)}) collective-permute-start(bf16[32,4096]{1,0:T(8,128)(2,1)} %fusion.25), channel_id=1, source_target_pairs={{0,32},{32,64},{64,96},{96,128},{128,160},{160,192},{192,224},{224... | collective-permute-start | bytes 786440 | tf_op jit(solution)/shard_map/ppermute | solution.py:13
  408.0 16.4 %collective-permute-start.25 = (bf16[32,4096]{1,0:T(8,128)(2,1)}, bf16[32,4096]{1,0:T(8,128)(2,1)}, u32[]{:S(2)}, u32[]{:S(2)}) collective-permute-start(bf16[32,4096]{1,0:T(8,128)(2,1)} %broadcast_select_fusion), channel_id=1, source_target_pairs={{0,64},{32,96},{64,128},{96,160},{128,192},{160,224},{192,256},{22... | collective-permute-start | bytes 786440 | tf_op jit(solution)/shard_map/ppermute | solution.py:13
  426.1 14.0 %collective-permute-start.26 = (bf16[32,4096]{1,0:T(8,128)(2,1)}, bf16[32,4096]{1,0:T(8,128)(2,1)}, u32[]{:S(2)}, u32[]{:S(2)}) collective-permute-start(bf16[32,4096]{1,0:T(8,128)(2,1)} %broadcast_select_fusion.1), channel_id=1, source_target_pairs={{0,128},{32,160},{64,192},{96,224},{128,256},{160,288},{192,320},{... | collective-permute-start | bytes 786440 | tf_op jit(solution)/shard_map/ppermute | solution.py:13
  441.8 17.1 %collective-permute-start.27 = (bf16[32,4096]{1,0:T(8,128)(2,1)}, bf16[32,4096]{1,0:T(8,128)(2,1)}, u32[]{:S(2)}, u32[]{:S(2)}) collective-permute-start(bf16[32,4096]{1,0:T(8,128)(2,1)} %broadcast_select_fusion.2), channel_id=1, source_target_pairs={{0,256},{32,288},{64,320},{96,352},{128,384},{160,416},{192,448},{... | collective-permute-start | bytes 786440 | tf_op jit(solution)/shard_map/ppermute | solution.py:13
  460.6 21.6 %collective-permute-start.28 = (bf16[32,4096]{1,0:T(8,128)(2,1)}, bf16[32,4096]{1,0:T(8,128)(2,1)}, u32[]{:S(2)}, u32[]{:S(2)}) collective-permute-start(bf16[32,4096]{1,0:T(8,128)(2,1)} %broadcast_select_fusion.3), channel_id=1, source_target_pairs={{0,512},{32,544},{64,576},{96,608},{128,640},{160,672},{192,704},{... | collective-permute-start | bytes 786440 | tf_op jit(solution)/shard_map/ppermute | solution.py:13
  487.5 16.0 %collective-permute-start.29 = (bf16[32,4096]{1,0:T(8,128)(2,1)S(1)}, bf16[32,4096]{1,0:T(8,128)(2,1)S(1)}, u32[]{:S(2)}, u32[]{:S(2)}) collective-permute-start(bf16[32,4096]{1,0:T(8,128)(2,1)S(1)} %bitcast.69), channel_id=1, source_target_pairs={{0,32},{32,64},{64,96},{96,128},{128,160},{160,192},{192,224},{224... | collective-permute-start | bytes 786440 | tf_op jit(solution)/shard_map/ppermute | solution.py:13
  503.5 16.1 %collective-permute-start.30 = (bf16[32,4096]{1,0:T(8,128)(2,1)S(1)}, bf16[32,4096]{1,0:T(8,128)(2,1)S(1)}, u32[]{:S(2)}, u32[]{:S(2)}) collective-permute-start(bf16[32,4096]{1,0:T(8,128)(2,1)S(1)} %broadcast_select_fusion.5), channel_id=1, source_target_pairs={{0,64},{32,96},{64,128},{96,160},{128,192},{160,224},{192,256},{22... | collective-permute-start | bytes 786440 | tf_op jit(solution)/shard_map/ppermute | solution.py:13
  519.6 13.7 %collective-permute-start.31 = (bf16[32,4096]{1,0:T(8,128)(2,1)S(1)}, bf16[32,4096]{1,0:T(8,128)(2,1)S(1)}, u32[]{:S(2)}, u32[]{:S(2)}) collective-permute-start(bf16[32,4096]{1,0:T(8,128)(2,1)S(1)} %broadcast_select_fusion.6), channel_id=1, source_target_pairs={{0,128},{32,160},{64,192},{96,224},{128,256},{160,288},{192,320},{... | collective-permute-start | bytes 786440 | tf_op jit(solution)/shard_map/ppermute | solution.py:13
  533.4 18.5 %collective-permute-start.32 = (bf16[32,4096]{1,0:T(8,128)(2,1)S(1)}, bf16[32,4096]{1,0:T(8,128)(2,1)S(1)}, u32[]{:S(2)}, u32[]{:S(2)}) collective-permute-start(bf16[32,4096]{1,0:T(8,128)(2,1)S(1)} %broadcast_select_fusion.7), channel_id=1, source_target_pairs={{0,256},{32,288},{64,320},{96,352},{128,384},{160,416},{192,448},{... | collective-permute-start | bytes 786440 | tf_op jit(solution)/shard_map/ppermute | solution.py:13
  552.0 20.8 %collective-permute-start.33 = (bf16[32,4096]{1,0:T(8,128)(2,1)S(1)}, bf16[32,4096]{1,0:T(8,128)(2,1)S(1)}, u32[]{:S(2)}, u32[]{:S(2)}) collective-permute-start(bf16[32,4096]{1,0:T(8,128)(2,1)S(1)} %broadcast_select_fusion.8), channel_id=1, source_target_pairs={{0,512},{32,544},{64,576},{96,608},{128,640},{160,672},{192,704},{... | collective-permute-start | bytes 786440 | tf_op jit(solution)/shard_map/ppermute | solution.py:13
  (5 other events, 265.1 us)
where the time goes:
time: 844 us; the launch traced here: 838 us
  waiting for transfers between devices  471 us (56%)
  blocking collectives  264 us (31%)
  starting transfers between devices  68.3 us (8%)
  other arithmetic  20.2 us (2%)
    ppermute x34, waiting for transfers between devices, passed_along(): return lax.ppermute(value, axis, pairs)  471 us
    psum x1, blocking collectives, per_device(): summed = lax.psum(gain_total, 'dp')  264 us
    ppermute x34, starting transfers between devices, passed_along(): return lax.ppermute(value, axis, pairs)  68.3 us
  transfers between devices with their start and end apart: 34, of which 34 were waited for; matrix products, arithmetic and copies ran while one was open for 0% of the time, Pallas kernels for 0%

commit v1 on v0

v1 whole, which is shorter than its diff:
```python
import jax
import jax.numpy as jnp
from jax import lax
from jax.sharding import PartitionSpec as P

HD = 256
STEPS = 3
LEAST_OFFSET = 3
CORES = 2
ROWS_Y = 4


def shifted(value, axis, steps):
    count = lax.axis_size(axis)
    pairs = [(source, (source + steps) % count) for source in range(count)]
    return lax.ppermute(value, axis, pairs)


def attend(queries, key_rows, value_rows, key_live):
    rows_here = queries.shape[0]
    width = queries.shape[1]
    heads_here = width // HD
    query_heads = queries.reshape(rows_here, heads_here, HD)
    key_heads = key_rows.reshape(key_rows.shape[0], heads_here, HD)
    value_heads = value_rows.reshape(value_rows.shape[0], heads_here, HD)
    scores = jnp.einsum(
        "qhd,khd->hqk", query_heads, key_heads, preferred_element_type=jnp.float32
    ) * HD ** (-0.5)
    scores = jnp.where(key_live[None, None, :], scores, jnp.float32(-1e30))
    top = jnp.max(scores, axis=-1, keepdims=True)
    expo = jnp.exp(scores - top)
    probs = (expo / jnp.sum(expo, axis=-1, keepdims=True)).astype(jnp.bfloat16)
    mixed = jnp.einsum("hqk,khd->qhd", probs, value_heads, preferred_element_type=jnp.float32)
    return mixed.reshape(rows_here, width).astype(jnp.bfloat16)


def normalized(state_wide):
    return (
        state_wide * lax.rsqrt(jnp.mean(state_wide * state_wide, axis=-1, keepdims=True) + 1e-06)
    ).astype(jnp.bfloat16)


def updated(state, gain, attended):
    return (
        state.astype(jnp.float32) + gain.astype(jnp.float32)[None, :] * attended.astype(jnp.float32)
    ).astype(jnp.bfloat16)


def dp_sum(row):
    count = lax.axis_size("dp")
    runs = count // ROWS_Y

    def partner(source, stage, j):
        y, rest = divmod(source, runs)
        run, core = divmod(rest, CORES)
        if stage == 0:
            core = (core + j) % CORES
        elif stage == 1:
            y = (y + j) % ROWS_Y
        else:
            run = (run + j) % (runs // CORES)
        return y * runs + run * CORES + core

    for stage, size in enumerate((CORES, ROWS_Y, runs // CORES)):
        arrived = [
            lax.ppermute(row, "dp", [(s, partner(s, stage, j)) for s in range(count)])
            for j in range(1, size)
        ]
        for piece in arrived:
            row = row + piece
    return row


def by_offset(offset_index, sections, send, *operands):
    def branch(offset):
        return lambda *values: send(offset, *values)

    return lax.switch(
        offset_index, [branch(c) for c in range(LEAST_OFFSET, sections)], *operands
    )


def to_owner(offset, states, gain, length):
    length_row = jnp.full((128,), length, jnp.int32).astype(jnp.bfloat16)
    return (
        shifted(states, "section", offset),
        shifted(jnp.concatenate([gain, length_row]), "section", offset),
        shifted(gain, "section", offset - 1),
    )


def from_owner(offset, *attended):
    return tuple(shifted(a, "section", t - offset) for t, a in enumerate(attended))


def per_device(states, memory, memory_len, decode_len, owner_map, section_gain, cotangent):
    sections = lax.axis_size("section")
    state, gain = states[0, 0], section_gain[0]
    keys, values = memory[0, 0, 0], memory[0, 0, 1]
    width = state.shape[1]
    key_live = jnp.arange(keys.shape[0]) < memory_len[0, 0]
    row_index = jnp.arange(state.shape[0])[:, None]
    offset_index = owner_map[0] - LEAST_OFFSET

    current, aux, gain_next = by_offset(
        offset_index, sections, to_owner, state, gain, decode_len[0, 0]
    )
    gains = [aux[:width], gain_next]
    live = row_index < aux[width].astype(jnp.int32)
    sent = []
    for t in range(STEPS):
        attended = attend(normalized(current.astype(jnp.float32)), keys, values, key_live)
        attended = jnp.where(live, attended, jnp.bfloat16(0))
        sent.append(attended)
        if t + 1 < STEPS:
            current = updated(current, gains[t], attended)
    sent = by_offset(offset_index, sections, from_owner, *sent)
    total = jnp.zeros((width,), jnp.float32)
    for t in range(STEPS):
        total = total + jnp.sum(
            cotangent[0, t, 0].astype(jnp.float32) * sent[t].astype(jnp.float32), axis=0
        )
    summed = dp_sum(total[None])
    for t in range(STEPS):
        state = updated(state, gain, sent[t])
        if t + 1 < STEPS:
            state = shifted(state, "section", 1)
    return (state[None, None], summed)


def solution(mesh):
    in_specs = (
        P("dp", "section", None, None),
        P("dp", "section", None, None, None),
        P("dp", "section"),
        P("dp", "section"),
        P(),
        P("section", None),
        P("dp", None, "section", None, None),
    )
    out_specs = (P("dp", "section", None, None), P("section", None))
    return jax.shard_map(
        per_device, mesh=mesh, in_specs=in_specs, out_specs=out_specs, check_vma=False
    )
```

time: 844 us -> 256 us (0.30)
  waiting for transfers between devices: 471 us -> 63 us
  blocking collectives: 264 us -> 0 us
  starting transfers between devices: 68.3 us -> 166 us
    ppermute x34 -> x15, waiting for transfers between devices: 471 us -> 63 us  [the longest x8 58.2 us: shifted(): return lax.ppermute(value, axis, pairs)]
    psum x1 -> x0, blocking collectives: 264 us -> none  [per_device(): summed = lax.psum(gain_total, 'dp')]
    ppermute x34 -> x15, starting transfers between devices: 68.3 us -> 166 us  [the longest x7 99.2 us: dp_sum(): lax.ppermute(row, 'dp', [(s, partner(s, stage, j)) for s in range(count)])]
    select_n x27 -> x1, other arithmetic: 13.5 us -> 0.09 us  [per_device(): attended = jnp.where(live, attended, jnp.bfloat16(0))]
  transfers between devices with their start and end apart: 34 -> 15, of which waited for: 34 -> 9; matrix products, arithmetic and copies ran while one was open for 0% -> 1% of each run, Pallas kernels for 0% -> 0%
where the time goes in v1:
time: 256 us; the launch traced here: 254 us
  starting transfers between devices  166 us (65%)
  waiting for transfers between devices  63 us (25%)
  other arithmetic  12.6 us (5%)
  local copies, waits for them, and re-layouts  4.58 us (2%)
  matrix products  3.64 us (1%)
  between operations  2.81 us (1%)
    ppermute x7, starting transfers between devices, dp_sum(): lax.ppermute(row, 'dp', [(s, partner(s, stage, j)) for s in range(count)])  99.2 us
    ppermute x8, starting transfers between devices, shifted(): return lax.ppermute(value, axis, pairs)  66.9 us
    ppermute x8, waiting for transfers between devices, shifted(): return lax.ppermute(value, axis, pairs)  58.2 us
  transfers between devices with their start and end apart: 15, of which 9 were waited for; matrix products, arithmetic and copies ran while one was open for 1% of the time, Pallas kernels for 0%

profile of v1, /device:TPU:1, one launch (start us, length us, event | category | flops | bytes accessed | tf_op | source)
XLA Modules:
  0.0 253.6 jit_solution(2798371174597431168)
XLA Ops:
  1.3 53.6 %conditional.8 = (bf16[4224]{0:T(1024)(128)(2,1)}, bf16[4096]{0:T(1024)(128)(2,1)}, f32[32,1]{0,1:T(1,128)S(1)}, bf16[32,4096]{1,0:T(8,128)(2,1)}) conditional(s32[]{:T(128)} %bitcast.60, (bf16[1,4096]{1,0:T(2,128)(2,1)}, s32[1,1]{1,0:T(1,128)}, bf16[32,4096]{1,0:T(8,128)(2,1)}) %tuple.908, ...), branch_computations={%region_0.2_spmd, %region_2.4_spmd, %region_4.6_spmd, %region_6.8_... | conditional | flops 393185 | bytes 1410594
  1.3 34.9 %collective-permute-start.164 = (bf16[32,4096]{1,0:T(8,128)(2,1)}, bf16[32,4096]{1,0:T(8,128)(2,1)}, u32[]{:S(2)}, u32[]{:S(2)}) collective-permute-start(bf16[32,4096]{1,0:T(8,128)(2,1)} %get-tuple-element.746), channel_id=1, source_target_pairs={{0,896},{32,928},{64,960},{96,992},{128,0},{160,32},{192,64},{224,... | collective-permute-start | bytes 786440 | tf_op jit(solution)/shard_map/cond/branch_25_fun/ppermute | solution.py:16
  37.1 12.6 %collective-permute-start.163 = (bf16[4096]{0:T(1024)(128)(2,1)S(1)}, bf16[4096]{0:T(1024)(128)(2,1)}, u32[]{:S(2)}, u32[]{:S(2)}) collective-permute-start(bf16[4096]{0:T(1024)(128)(2,1)S(1)} %reduce.25), channel_id=1, source_target_pairs={{0,864},{32,896},{64,928},{96,960},{128,992},{160,0},{192,32},{224... | collective-permute-start | bytes 24584 | tf_op jit(solution)/shard_map/cond/branch_25_fun/ppermute | solution.py:16
  50.4 2.8 %collective-permute-start.162 = (bf16[4224]{0:T(1024)(128)(2,1)S(1)}, bf16[4224]{0:T(1024)(128)(2,1)}, u32[]{:S(2)}, u32[]{:S(2)}) collective-permute-start(bf16[4224]{0:T(1024)(128)(2,1)S(1)} %concatenate.83), channel_id=1, source_target_pairs={{0,896},{32,928},{64,960},{96,992},{128,0},{160,32},{192,64},{224,... | collective-permute-start | bytes 25352 | tf_op jit(solution)/shard_map/cond/branch_25_fun/ppermute | solution.py:16
  53.2 1.1 multiply_reduce_fusion.25
  55.6 1.3 slice.25
  57.6 1.7 fusion.44
  61.3 1.1 fusion.17
  62.9 0.9 fusion.6
  65.2 1.3 fusion.27
  70.0 40.4 %conditional.9 = (bf16[32,4096]{1,0:T(8,128)(2,1)}, bf16[32,4096]{1,0:T(8,128)(2,1)}, bf16[32,4096]{1,0:T(8,128)(2,1)}) conditional(s32[]{:T(128)} %bitcast.60, (bf16[32,4096]{1,0:T(8,128)(2,1)S(1)}, bf16[32,4096]{1,0:T(8,128)(2,1)S(1)}, pred[32]{0:T(512)(128)(4,1)S(1)}, bf16[32,16,256]{2,0,1:T(8,128)(2,1)S(1)}, ...), branch_computations={%region_66.67_spmd, %region_67.68_spmd, %region_68.69_spmd, %regio... | conditional | flops 131072 | bytes 4980912
  70.1 3.5 %collective-permute-start.75 = (bf16[32,4096]{1,0:T(8,128)(2,1)S(1)}, bf16[32,4096]{1,0:T(8,128)(2,1)}, u32[]{:S(2)}, u32[]{:S(2)}) collective-permute-start(bf16[32,4096]{1,0:T(8,128)(2,1)S(1)} %get-tuple-element.881), channel_id=1, source_target_pairs={{0,128},{32,160},{64,192},{96,224},{128,256},{160,288},{192,320},{... | collective-permute-start | bytes 786440 | tf_op jit(solution)/shard_map/cond/branch_25_fun/ppermute | solution.py:16
  73.6 1.9 collective-permute-start.76
  75.9 2.1 collective-permute-start.77
  78.0 6.9 %collective-permute-done.75 = bf16[32,4096]{1,0:T(8,128)(2,1)} collective-permute-done((bf16[32,4096]{1,0:T(8,128)(2,1)S(1)}, bf16[32,4096]{1,0:T(8,128)(2,1)}, u32[]{:S(2)}, u32[]{:S(2)}) %collective-permute-start.75) | collective-permute-done | bytes 262176 | tf_op jit(solution)/shard_map/cond/branch_25_fun/ppermute | solution.py:16
  84.8 25.6 %collective-permute-done.76 = bf16[32,4096]{1,0:T(8,128)(2,1)} collective-permute-done((bf16[32,4096]{1,0:T(8,128)(2,1)S(1)}, bf16[32,4096]{1,0:T(8,128)(2,1)}, u32[]{:S(2)}, u32[]{:S(2)}) %collective-permute-start.76) | collective-permute-done | bytes 262176 | tf_op jit(solution)/shard_map/cond/branch_25_fun/ppermute | solution.py:16
  110.5 1.1 fusion.20
  111.6 7.1 %collective-permute-start.174 = (bf16[32,4096]{1,0:T(8,128)(2,1)S(1)}, bf16[32,4096]{1,0:T(8,128)(2,1)S(1)}, u32[]{:S(2)}, u32[]{:S(2)}) collective-permute-start(bf16[32,4096]{1,0:T(8,128)(2,1)S(1)} %fusion.20), channel_id=1, source_target_pairs={{0,32},{32,64},{64,96},{96,128},{128,160},{160,192},{192,224},{224... | collective-permute-start | bytes 786440 | tf_op jit(solution)/shard_map/ppermute | solution.py:16
  118.7 10.5 %collective-permute-done.174 = bf16[32,4096]{1,0:T(8,128)(2,1)S(1)} collective-permute-done((bf16[32,4096]{1,0:T(8,128)(2,1)S(1)}, bf16[32,4096]{1,0:T(8,128)(2,1)S(1)}, u32[]{:S(2)}, u32[]{:S(2)}) %collective-permute-start.174) | collective-permute-done | bytes 262176 | tf_op jit(solution)/shard_map/ppermute | solution.py:16
  129.2 1.0 fusion.23
  130.2 1.9 collective-permute-start.175
  132.1 14.7 %collective-permute-done.175 = bf16[32,4096]{1,0:T(8,128)(2,1)S(1)} collective-permute-done((bf16[32,4096]{1,0:T(8,128)(2,1)S(1)}, bf16[32,4096]{1,0:T(8,128)(2,1)S(1)}, u32[]{:S(2)}, u32[]{:S(2)}) %collective-permute-start.175) | collective-permute-done | bytes 262176 | tf_op jit(solution)/shard_map/ppermute | solution.py:16
  146.8 2.1 fusion.21
  148.9 4.6 %collective-permute-start.176 = (f32[1,4096]{1,0:T(1,128)S(1)}, f32[1,4096]{1,0:T(1,128)S(1)}, u32[]{:S(2)}, u32[]{:S(2)}) collective-permute-start(f32[1,4096]{1,0:T(1,128)S(1)} %bitcast.276), channel_id=1, source_target_pairs={{0,1},{1,0},{2,3},{3,2},{4,5},{5,4},{6,7},{7,6},{8,9},{9,8},{10,11... | collective-permute-start | bytes 49160 | tf_op jit(solution)/shard_map/ppermute | solution.py:66
  154.3 20.8 %collective-permute-start.179 = (f32[1,4096]{1,0:T(1,128)S(1)}, f32[1,4096]{1,0:T(1,128)S(1)}, u32[]{:S(2)}, u32[]{:S(2)}) collective-permute-start(f32[1,4096]{1,0:T(1,128)S(1)} %add.152), channel_id=1, source_target_pairs={{0,24},{1,25},{2,26},{3,27},{4,28},{5,29},{6,30},{7,31},{8,0},{9,1... | collective-permute-start | bytes 49160 | tf_op jit(solution)/shard_map/ppermute | solution.py:66
  175.1 30.8 %collective-permute-start.178 = (f32[1,4096]{1,0:T(1,128)S(1)}, f32[1,4096]{1,0:T(1,128)S(1)}, u32[]{:S(2)}, u32[]{:S(2)}) collective-permute-start(f32[1,4096]{1,0:T(1,128)S(1)} %add.152), channel_id=1, source_target_pairs={{0,16},{1,17},{2,18},{3,19},{4,20},{5,21},{6,22},{7,23},{8,24},{9,... | collective-permute-start | bytes 49160 | tf_op jit(solution)/shard_map/ppermute | solution.py:66
  205.9 3.3 %collective-permute-start.177 = (f32[1,4096]{1,0:T(1,128)S(1)}, f32[1,4096]{1,0:T(1,128)S(1)}, u32[]{:S(2)}, u32[]{:S(2)}) collective-permute-start(f32[1,4096]{1,0:T(1,128)S(1)} %add.152), channel_id=1, source_target_pairs={{0,8},{1,9},{2,10},{3,11},{4,12},{5,13},{6,14},{7,15},{8,16},{9,17... | collective-permute-start | bytes 49160 | tf_op jit(solution)/shard_map/ppermute | solution.py:66
  209.9 1.7 collective-permute-done.177
  211.6 18.3 %collective-permute-start.182 = (f32[1,4096]{1,0:T(1,128)S(1)}, f32[1,4096]{1,0:T(1,128)S(1)}, u32[]{:S(2)}, u32[]{:S(2)}) collective-permute-start(f32[1,4096]{1,0:T(1,128)S(1)} %add_add_fusion.1), channel_id=1, source_target_pairs={{0,6},{1,7},{2,0},{3,1},{4,2},{5,3},{6,4},{7,5},{8,14},{9,15},{10,... | collective-permute-start | bytes 49160 | tf_op jit(solution)/shard_map/ppermute | solution.py:66
  230.0 9.4 %collective-permute-start.181 = (f32[1,4096]{1,0:T(1,128)S(1)}, f32[1,4096]{1,0:T(1,128)S(1)}, u32[]{:S(2)}, u32[]{:S(2)}) collective-permute-start(f32[1,4096]{1,0:T(1,128)S(1)} %add_add_fusion.1), channel_id=1, source_target_pairs={{0,4},{1,5},{2,6},{3,7},{4,0},{5,1},{6,2},{7,3},{8,12},{9,13},{10,... | collective-permute-start | bytes 49160 | tf_op jit(solution)/shard_map/ppermute | solution.py:66
  239.3 12.1 %collective-permute-start.180 = (f32[1,4096]{1,0:T(1,128)S(1)}, f32[1,4096]{1,0:T(1,128)S(1)}, u32[]{:S(2)}, u32[]{:S(2)}) collective-permute-start(f32[1,4096]{1,0:T(1,128)S(1)} %add_add_fusion.1), channel_id=1, source_target_pairs={{0,2},{1,3},{2,4},{3,5},{4,6},{5,7},{6,0},{7,1},{8,10},{9,11},{10,... | collective-permute-start | bytes 49160 | tf_op jit(solution)/shard_map/ppermute | solution.py:66
  251.4 1.5 collective-permute-done.181
  (46 shorter events, 11.4 us)
Async XLA Ops:
  1.3 51.9 %collective-permute-start.164 = (bf16[32,4096]{1,0:T(8,128)(2,1)}, bf16[32,4096]{1,0:T(8,128)(2,1)}, u32[]{:S(2)}, u32[]{:S(2)}) collective-permute-start(bf16[32,4096]{1,0:T(8,128)(2,1)} %get-tuple-element.746), channel_id=1, source_target_pairs={{0,896},{32,928},{64,960},{96,992},{128,0},{160,32},{192,64},{224,... | collective-permute-start | bytes 786440 | tf_op jit(solution)/shard_map/cond/branch_25_fun/ppermute | solution.py:16
  37.1 17.3 %collective-permute-start.163 = (bf16[4096]{0:T(1024)(128)(2,1)S(1)}, bf16[4096]{0:T(1024)(128)(2,1)}, u32[]{:S(2)}, u32[]{:S(2)}) collective-permute-start(bf16[4096]{0:T(1024)(128)(2,1)S(1)} %reduce.25), channel_id=1, source_target_pairs={{0,864},{32,896},{64,928},{96,960},{128,992},{160,0},{192,32},{224... | collective-permute-start | bytes 24584 | tf_op jit(solution)/shard_map/cond/branch_25_fun/ppermute | solution.py:16
  50.4 4.5 %collective-permute-start.162 = (bf16[4224]{0:T(1024)(128)(2,1)S(1)}, bf16[4224]{0:T(1024)(128)(2,1)}, u32[]{:S(2)}, u32[]{:S(2)}) collective-permute-start(bf16[4224]{0:T(1024)(128)(2,1)S(1)} %concatenate.83), channel_id=1, source_target_pairs={{0,896},{32,928},{64,960},{96,992},{128,0},{160,32},{192,64},{224,... | collective-permute-start | bytes 25352 | tf_op jit(solution)/shard_map/cond/branch_25_fun/ppermute | solution.py:16
  70.0 40.5 %copy-start.1 = (bf16[1,1,32,4096]{3,2,1,0:T(8,128)(2,1)S(1)}, bf16[1,1,32,4096]{3,2,1,0:T(8,128)(2,1)}, u32[]{:S(2)}) copy-start(bf16[1,1,32,4096]{3,2,1,0:T(8,128)(2,1)} %param.65) | copy-start | bytes 786436
  70.1 14.7 %collective-permute-start.75 = (bf16[32,4096]{1,0:T(8,128)(2,1)S(1)}, bf16[32,4096]{1,0:T(8,128)(2,1)}, u32[]{:S(2)}, u32[]{:S(2)}) collective-permute-start(bf16[32,4096]{1,0:T(8,128)(2,1)S(1)} %get-tuple-element.881), channel_id=1, source_target_pairs={{0,128},{32,160},{64,192},{96,224},{128,256},{160,288},{192,320},{... | collective-permute-start | bytes 786440 | tf_op jit(solution)/shard_map/cond/branch_25_fun/ppermute | solution.py:16
  73.6 36.9 %collective-permute-start.76 = (bf16[32,4096]{1,0:T(8,128)(2,1)S(1)}, bf16[32,4096]{1,0:T(8,128)(2,1)}, u32[]{:S(2)}, u32[]{:S(2)}) collective-permute-start(bf16[32,4096]{1,0:T(8,128)(2,1)S(1)} %get-tuple-element.882), channel_id=1, source_target_pairs={{0,160},{32,192},{64,224},{96,256},{128,288},{160,320},{192,352},{... | collective-permute-start | bytes 786440 | tf_op jit(solution)/shard_map/cond/branch_25_fun/ppermute | solution.py:16
  75.9 34.6 %collective-permute-start.77 = (bf16[32,4096]{1,0:T(8,128)(2,1)S(1)}, bf16[32,4096]{1,0:T(8,128)(2,1)}, u32[]{:S(2)}, u32[]{:S(2)}) collective-permute-start(bf16[32,4096]{1,0:T(8,128)(2,1)S(1)} %broadcast_select_fusion.25), channel_id=1, source_target_pairs={{0,192},{32,224},{64,256},{96,288},{128,320},{160,352},{192,384},{... | collective-permute-start | bytes 786440 | tf_op jit(solution)/shard_map/cond/branch_25_fun/ppermute | solution.py:16
  110.5 36.4 %copy-start = (bf16[1,3,1,32,4096]{4,3,2,1,0:T(8,128)(2,1)S(1)}, bf16[1,3,1,32,4096]{4,3,2,1,0:T(8,128)(2,1)}, u32[]{:S(2)}) copy-start(bf16[1,3,1,32,4096]{4,3,2,1,0:T(8,128)(2,1)} %param.71) | copy-start | bytes 2359300
  111.6 17.6 %collective-permute-start.174 = (bf16[32,4096]{1,0:T(8,128)(2,1)S(1)}, bf16[32,4096]{1,0:T(8,128)(2,1)S(1)}, u32[]{:S(2)}, u32[]{:S(2)}) collective-permute-start(bf16[32,4096]{1,0:T(8,128)(2,1)S(1)} %fusion.20), channel_id=1, source_target_pairs={{0,32},{32,64},{64,96},{96,128},{128,160},{160,192},{192,224},{224... | collective-permute-start | bytes 786440 | tf_op jit(solution)/shard_map/ppermute | solution.py:16
  130.2 16.6 %collective-permute-start.175 = (bf16[32,4096]{1,0:T(8,128)(2,1)S(1)}, bf16[32,4096]{1,0:T(8,128)(2,1)S(1)}, u32[]{:S(2)}, u32[]{:S(2)}) collective-permute-start(bf16[32,4096]{1,0:T(8,128)(2,1)S(1)} %fusion.23), channel_id=1, source_target_pairs={{0,32},{32,64},{64,96},{96,128},{128,160},{160,192},{192,224},{224... | collective-permute-start | bytes 786440 | tf_op jit(solution)/shard_map/ppermute | solution.py:16
  148.9 5.4 %collective-permute-start.176 = (f32[1,4096]{1,0:T(1,128)S(1)}, f32[1,4096]{1,0:T(1,128)S(1)}, u32[]{:S(2)}, u32[]{:S(2)}) collective-permute-start(f32[1,4096]{1,0:T(1,128)S(1)} %bitcast.276), channel_id=1, source_target_pairs={{0,1},{1,0},{2,3},{3,2},{4,5},{5,4},{6,7},{7,6},{8,9},{9,8},{10,11... | collective-permute-start | bytes 49160 | tf_op jit(solution)/shard_map/ppermute | solution.py:66
  154.3 54.9 %collective-permute-start.179 = (f32[1,4096]{1,0:T(1,128)S(1)}, f32[1,4096]{1,0:T(1,128)S(1)}, u32[]{:S(2)}, u32[]{:S(2)}) collective-permute-start(f32[1,4096]{1,0:T(1,128)S(1)} %add.152), channel_id=1, source_target_pairs={{0,24},{1,25},{2,26},{3,27},{4,28},{5,29},{6,30},{7,31},{8,0},{9,1... | collective-permute-start | bytes 49160 | tf_op jit(solution)/shard_map/ppermute | solution.py:66
  175.1 34.8 %collective-permute-start.178 = (f32[1,4096]{1,0:T(1,128)S(1)}, f32[1,4096]{1,0:T(1,128)S(1)}, u32[]{:S(2)}, u32[]{:S(2)}) collective-permute-start(f32[1,4096]{1,0:T(1,128)S(1)} %add.152), channel_id=1, source_target_pairs={{0,16},{1,17},{2,18},{3,19},{4,20},{5,21},{6,22},{7,23},{8,24},{9,... | collective-permute-start | bytes 49160 | tf_op jit(solution)/shard_map/ppermute | solution.py:66
  205.9 5.7 %collective-permute-start.177 = (f32[1,4096]{1,0:T(1,128)S(1)}, f32[1,4096]{1,0:T(1,128)S(1)}, u32[]{:S(2)}, u32[]{:S(2)}) collective-permute-start(f32[1,4096]{1,0:T(1,128)S(1)} %add.152), channel_id=1, source_target_pairs={{0,8},{1,9},{2,10},{3,11},{4,12},{5,13},{6,14},{7,15},{8,16},{9,17... | collective-permute-start | bytes 49160 | tf_op jit(solution)/shard_map/ppermute | solution.py:66
  211.6 39.8 %collective-permute-start.182 = (f32[1,4096]{1,0:T(1,128)S(1)}, f32[1,4096]{1,0:T(1,128)S(1)}, u32[]{:S(2)}, u32[]{:S(2)}) collective-permute-start(f32[1,4096]{1,0:T(1,128)S(1)} %add_add_fusion.1), channel_id=1, source_target_pairs={{0,6},{1,7},{2,0},{3,1},{4,2},{5,3},{6,4},{7,5},{8,14},{9,15},{10,... | collective-permute-start | bytes 49160 | tf_op jit(solution)/shard_map/ppermute | solution.py:66
  230.0 23.0 %collective-permute-start.181 = (f32[1,4096]{1,0:T(1,128)S(1)}, f32[1,4096]{1,0:T(1,128)S(1)}, u32[]{:S(2)}, u32[]{:S(2)}) collective-permute-start(f32[1,4096]{1,0:T(1,128)S(1)} %add_add_fusion.1), channel_id=1, source_target_pairs={{0,4},{1,5},{2,6},{3,7},{4,0},{5,1},{6,2},{7,3},{8,12},{9,13},{10,... | collective-permute-start | bytes 49160 | tf_op jit(solution)/shard_map/ppermute | solution.py:66
  239.3 13.6 %collective-permute-start.180 = (f32[1,4096]{1,0:T(1,128)S(1)}, f32[1,4096]{1,0:T(1,128)S(1)}, u32[]{:S(2)}, u32[]{:S(2)}) collective-permute-start(f32[1,4096]{1,0:T(1,128)S(1)} %add_add_fusion.1), channel_id=1, source_target_pairs={{0,2},{1,3},{2,4},{3,5},{4,6},{5,7},{6,0},{7,1},{8,10},{9,11},{10,... | collective-permute-start | bytes 49160 | tf_op jit(solution)/shard_map/ppermute | solution.py:66

commit v2 on v0

v2 whole, which is shorter than its diff:
```python
import functools

import jax
import jax.numpy as jnp
from jax import lax
from jax.experimental import pallas as pl
from jax.experimental.pallas import tpu as pltpu
from jax.sharding import PartitionSpec as P

HD = 256
STEPS = 3
LEAST_OFFSET = 3
LANES = 128
CORES = 2
ROWS_Y = 4
VMEM = pl.BlockSpec(memory_space=pltpu.VMEM)
SMEM = pl.BlockSpec(memory_space=pltpu.SMEM)


def shifted(value, axis, steps):
    count = lax.axis_size(axis)
    pairs = [(source, (source + steps) % count) for source in range(count)]
    return lax.ppermute(value, axis, pairs)


def pack_kernel(length_ref, state_ref, gain_ref, message_ref):
    blocks = state_ref.shape[1] // LANES
    for b in range(blocks):
        message_ref[b] = state_ref[:, b * LANES : (b + 1) * LANES]
    wide = gain_ref[...].astype(jnp.float32)
    rows = [wide[:, b * LANES : (b + 1) * LANES] for b in range(blocks)]
    message_ref[blocks] = jnp.concatenate(rows, axis=0).astype(jnp.bfloat16)
    length = jnp.full(message_ref.shape[1:], length_ref[0], jnp.int32)
    message_ref[blocks + 1] = length.astype(jnp.float32).astype(jnp.bfloat16)


def packed(states, gain, length):
    rows, width = states.shape
    blocks = width // LANES
    return pl.pallas_call(
        pack_kernel,
        out_shape=jax.ShapeDtypeStruct((blocks + 2, rows, LANES), states.dtype),
        in_specs=[SMEM, VMEM, VMEM],
        out_specs=VMEM,
        name="pack",
    )(length, states, gain)


def steps_kernel(key_len_ref, message_ref, gain_next_ref, memory_ref, *refs):
    out_refs, (score_ref, state_ref) = refs[:STEPS], refs[STEPS:]
    rows = message_ref.shape[1]
    width = memory_ref.shape[2]
    heads, keys = width // HD, memory_ref.shape[1]
    blocks = width // LANES
    per_head = HD // LANES
    key_live = lax.broadcasted_iota(jnp.int32, (rows, keys), 1) < key_len_ref[0]
    length = message_ref[blocks + 1][:, :1].astype(jnp.float32)
    row_live = lax.broadcasted_iota(jnp.int32, (rows, 1), 0).astype(jnp.float32) < length
    for t in range(STEPS):
        source = message_ref if t == 0 else state_ref
        squares = jnp.zeros((rows, LANES), jnp.float32)
        for b in range(blocks):
            wide = source[b].astype(jnp.float32)
            squares = squares + wide * wide
        mean = jnp.sum(squares, axis=1, keepdims=True) / width
        scale = lax.rsqrt(mean + 1e-06)
        for h in range(heads):
            query = jnp.concatenate(
                [
                    (source[h * per_head + j].astype(jnp.float32) * scale).astype(jnp.bfloat16)
                    for j in range(per_head)
                ],
                axis=1,
            )
            scores = lax.dot_general(
                query,
                memory_ref[0, :, h * HD : (h + 1) * HD],
                (((1,), (1,)), ((), ())),
                preferred_element_type=jnp.float32,
            )
            score_ref[h] = jnp.where(key_live, scores * HD ** (-0.5), jnp.float32(-1e30))
        for h in range(heads):
            scores = score_ref[h]
            expo = jnp.exp(scores - jnp.max(scores, axis=1, keepdims=True))
            probs = (expo / jnp.sum(expo, axis=1, keepdims=True)).astype(jnp.bfloat16)
            mixed = jnp.dot(
                probs,
                memory_ref[1, :, h * HD : (h + 1) * HD],
                preferred_element_type=jnp.float32,
            ).astype(jnp.bfloat16)
            mixed = jnp.where(row_live, mixed.astype(jnp.float32), 0.0)
            out_refs[t][:, h * HD : (h + 1) * HD] = mixed.astype(jnp.bfloat16)
            if t + 1 < STEPS:
                for j in range(per_head):
                    b = h * per_head + j
                    if t == 0:
                        gain = message_ref[blocks][b : b + 1, :]
                    else:
                        gain = gain_next_ref[:, b * LANES : (b + 1) * LANES]
                    state_ref[b] = (
                        source[b].astype(jnp.float32)
                        + gain.astype(jnp.float32) * mixed[:, j * LANES : (j + 1) * LANES]
                    ).astype(jnp.bfloat16)


def attended_steps(message, gain_next, memory, key_len):
    rows = message.shape[1]
    keys, width = memory.shape[1:]
    return pl.pallas_call(
        steps_kernel,
        out_shape=[jax.ShapeDtypeStruct((rows, width), jnp.bfloat16)] * STEPS,
        in_specs=[SMEM, VMEM, VMEM, VMEM],
        out_specs=[VMEM] * STEPS,
        scratch_shapes=[
            pltpu.VMEM((width // HD, rows, keys), jnp.float32),
            pltpu.VMEM((width // LANES, rows, LANES), jnp.bfloat16),
        ],
        compiler_params=pltpu.CompilerParams(vmem_limit_bytes=16 << 20),
        name="steps",
    )(key_len, message, gain_next, memory)


def updated(state, gain, attended):
    return (
        state.astype(jnp.float32) + gain.astype(jnp.float32) * attended.astype(jnp.float32)
    ).astype(jnp.bfloat16)


def by_offset(offset_index, sections, send, *operands):
    return lax.switch(
        offset_index,
        [functools.partial(send, c) for c in range(LEAST_OFFSET, sections)],
        *operands,
    )


def to_owner(offset, message, gain):
    return shifted(message, "section", offset), shifted(gain, "section", offset - 1)


def from_owner(offset, *attended):
    return tuple(shifted(a, "section", t - offset) for t, a in enumerate(attended))


def near_dp_sum(row):
    count = lax.axis_size("dp")
    runs = count // (ROWS_Y * CORES)
    groups = [
        [(y * runs + run) * CORES + core for y in range(ROWS_Y) for core in range(CORES)]
        for run in range(runs)
    ]
    copies = jnp.broadcast_to(row, (ROWS_Y * CORES, row.shape[1]))
    return jnp.sum(
        lax.all_to_all(copies, "dp", 0, 0, axis_index_groups=groups), axis=0, keepdims=True
    )


def from_run(row, step):
    count = lax.axis_size("dp")
    runs = count // (ROWS_Y * CORES)

    def target(source):
        y, rest = divmod(source, runs * CORES)
        run, core = divmod(rest, CORES)
        return (y * runs + (run + step) % runs) * CORES + core

    return lax.ppermute(row, "dp", [(s, target(s)) for s in range(count)])


def per_device(states, memory, memory_len, decode_len, owner_map, section_gain, cotangent):
    sections = lax.axis_size("section")
    runs = lax.axis_size("dp") // (ROWS_Y * CORES)
    state, gain = states[0, 0], section_gain
    offset_index = owner_map[0] - LEAST_OFFSET

    message = packed(state, gain, decode_len[0])
    message, gain_next = by_offset(offset_index, sections, to_owner, message, gain)
    sent = attended_steps(message, gain_next, memory[0, 0], memory_len[0])
    sent = by_offset(offset_index, sections, from_owner, *sent)

    total = jnp.zeros((1, state.shape[1]), jnp.float32)
    for t in range(STEPS):
        total = total + jnp.sum(
            cotangent[0, t, 0].astype(jnp.float32) * sent[t].astype(jnp.float32),
            axis=0,
            keepdims=True,
        )
    total, state = lax.optimization_barrier((total, updated(state, gain, sent[0])))
    state = shifted(state, "section", 1)
    total = near_dp_sum(total)
    arrived = [from_run(total, step) for step in range(1, runs)]
    state = shifted(updated(state, gain, sent[1]), "section", 1)
    state = updated(state, gain, sent[2])
    return (state[None, None], sum(arrived, total))


def solution(mesh):
    in_specs = (
        P("dp", "section", None, None),
        P("dp", "section", None, None, None),
        P("dp", "section"),
        P("dp", "section"),
        P(),
        P("section", None),
        P("dp", None, "section", None, None),
    )
    out_specs = (P("dp", "section", None, None), P("section", None))
    return jax.shard_map(
        per_device, mesh=mesh, in_specs=in_specs, out_specs=out_specs, check_vma=False
    )
```

time: 844 us -> 167 us (0.20)
  waiting for transfers between devices: 471 us -> 56.3 us
  blocking collectives: 264 us -> 10.8 us
  starting transfers between devices: 68.3 us -> 84.6 us
  other arithmetic: 20.2 us -> 5.72 us
    ppermute x34 -> x10, waiting for transfers between devices: 471 us -> 56.3 us  [the longest x7 54.1 us: shifted(): return lax.ppermute(value, axis, pairs)]
    psum x1 -> x0, blocking collectives: 264 us -> none  [per_device(): summed = lax.psum(gain_total, 'dp')]
    ppermute x34 -> x10, starting transfers between devices: 68.3 us -> 84.6 us  [the longest x7 48.7 us: shifted(): return lax.ppermute(value, axis, pairs)]
    select_n x27 -> x0, other arithmetic: 13.5 us -> none  [the longest x15 10.3 us: per_device(): routed = jnp.where(distance >> level & 1 == 1, arrived, routed)]
    all_to_all x0 -> x1, blocking collectives: none -> 10.8 us  [near_dp_sum(): lax.all_to_all(copies, 'dp', 0, 0, axis_index_groups=groups)]
  transfers between devices with their start and end apart: 34 -> 10, of which waited for: 34 -> 4; matrix products, arithmetic and copies ran while one was open for 0% -> 1% of each run, Pallas kernels for 0% -> 0%
where the time goes in v2:
time: 167 us
  starting transfers between devices  84.6 us (51%)
  waiting for transfers between devices  56.3 us (34%)
  blocking collectives  10.8 us (6%)
  other arithmetic  5.72 us (3%)
  Pallas kernels  4.64 us (3%)
  between operations  2.73 us (2%)
  local copies, waits for them, and re-layouts  1.67 us (1%)
    ppermute x7, waiting for transfers between devices, shifted(): return lax.ppermute(value, axis, pairs)  54.1 us
    ppermute x7, starting transfers between devices, shifted(): return lax.ppermute(value, axis, pairs)  48.7 us
    ppermute x3, starting transfers between devices, from_run(): return lax.ppermute(row, 'dp', [(s, target(s)) for s in range(count)])  35.9 us
    all_to_all x1, blocking collectives, near_dp_sum(): lax.all_to_all(copies, 'dp', 0, 0, axis_index_groups=groups)  10.8 us
    pallas_call x1, Pallas kernels, attended_steps(): pl.pallas_call(steps_kernel, out_shape=[jax.ShapeDtypeStruct((rows, width...  3.63 us
  transfers between devices with their start and end apart: 10, of which 4 were waited for; matrix products, arithmetic and copies ran while one was open for 1% of the time, Pallas kernels for 0%

profile of v2, /device:TPU:1, one launch (start us, length us, event | category | flops | bytes accessed | tf_op | source)
XLA Modules:
  0.0 166.6 jit_solution(686946542868354531)
XLA Ops:
  0.6 0.0 copy-start.1
  1.3 0.7 mul.43
  2.1 1.0 pack.1
  4.4 19.2 %conditional.4 = (bf16[34,32,128]{2,1,0:T(8,128)(2,1)}, bf16[1,4096]{1,0:T(2,128)(2,1)}) conditional(s32[]{:T(128)} %bitcast.1, (bf16[34,32,128]{2,1,0:T(8,128)(2,1)S(1)}, bf16[1,4096]{1,0:T(2,128)(2,1)}) %tuple.446, (bf16[34,32,128]{2,1,0:T(8,128)(2,1)S(1)}, bf16[1,4096]{1,0:T(2,128)(2,1)}) %tuple.446, ...), branch_computations={%region_0.0_spmd, %region_1.0_spmd, %region_2.0_spmd, %region_3.0_... | conditional | bytes 1146976 | solution.py:130
  4.4 12.4 %collective-permute-start.42 = (bf16[34,32,128]{2,1,0:T(8,128)(2,1)S(1)}, bf16[34,32,128]{2,1,0:T(8,128)(2,1)}, u32[]{:S(2)}, u32[]{:S(2)}) collective-permute-start(bf16[34,32,128]{2,1,0:T(8,128)(2,1)S(1)} %get-tuple-element.350), channel_id=1, source_target_pairs={{0,768},{32,800},{64,832},{96,864},{128,896},{160,928},{192,960},{... | collective-permute-start | bytes 835592 | tf_op jit(solution)/shard_map/cond/branch_21_fun/ppermute | solution.py:23
  16.8 2.8 %collective-permute-start.43 = (bf16[1,4096]{1,0:T(2,128)(2,1)}, bf16[1,4096]{1,0:T(2,128)(2,1)}, u32[]{:S(2)}, u32[]{:S(2)}) collective-permute-start(bf16[1,4096]{1,0:T(2,128)(2,1)} %get-tuple-element.351), channel_id=1, source_target_pairs={{0,736},{32,768},{64,800},{96,832},{128,864},{160,896},{192,928},{... | collective-permute-start | bytes 24584 | tf_op jit(solution)/shard_map/cond/branch_21_fun/ppermute | solution.py:23
  19.5 4.0 %collective-permute-done.43 = bf16[1,4096]{1,0:T(2,128)(2,1)} collective-permute-done((bf16[1,4096]{1,0:T(2,128)(2,1)}, bf16[1,4096]{1,0:T(2,128)(2,1)}, u32[]{:S(2)}, u32[]{:S(2)}) %collective-permute-start.43) | collective-permute-done | bytes 8224 | tf_op jit(solution)/shard_map/cond/branch_21_fun/ppermute | solution.py:23
  23.6 0.0 collective-permute-done.42
  23.6 1.6 copy-done
  25.2 3.6 %steps.1 = (bf16[32,4096]{1,0:T(8,128)(2,1)S(1)}, bf16[32,4096]{1,0:T(8,128)(2,1)S(1)}, bf16[32,4096]{1,0:T(8,128)(2,1)S(1)}) custom-call(s32[1]{0:T(128)} %bitcast.22.key_len_ref, bf16[34,32,128]{2,1,0:T(8,128)(2,1)} %get-tuple-element.462.message_ref, bf16[1,4096]{1,0:T(2,128)(2,1)} %get-tuple-element.463.gain_next_ref, bf16[2,128,4096]{2,1,0:T(8,128)(2,1)S(1)} %bitcast.24), custom_call_target="tpu_custom_call" | custom-call | tf_op jit(solution)/shard_map/steps/pallas_call | solution.py:109
  28.8 61.5 %conditional.6 = (bf16[32,4096]{1,0:T(8,128)(2,1)}, bf16[32,4096]{1,0:T(8,128)(2,1)}, bf16[32,4096]{1,0:T(8,128)(2,1)}) conditional(s32[]{:T(128)} %bitcast.1, (bf16[32,4096]{1,0:T(8,128)(2,1)S(1)}, bf16[32,4096]{1,0:T(8,128)(2,1)S(1)}, bf16[32,4096]{1,0:T(8,128)(2,1)S(1)}) %steps.1, (bf16[32,4096]{1,0:T(8,128)(2,1)S(1)}, ...), branch_computations={%region_29.0_spmd, %region_30.0_spmd, %region_31.0_spmd, %region_3... | conditional | bytes 3145872
  28.8 6.6 %collective-permute-start.121 = (bf16[32,4096]{1,0:T(8,128)(2,1)S(1)}, bf16[32,4096]{1,0:T(8,128)(2,1)}, u32[]{:S(2)}, u32[]{:S(2)}) collective-permute-start(bf16[32,4096]{1,0:T(8,128)(2,1)S(1)} %get-tuple-element.429), channel_id=1, source_target_pairs={{0,256},{32,288},{64,320},{96,352},{128,384},{160,416},{192,448},{... | collective-permute-start | bytes 786440 | tf_op jit(solution)/shard_map/cond/branch_21_fun/ppermute | solution.py:23
  35.4 5.8 %collective-permute-start.122 = (bf16[32,4096]{1,0:T(8,128)(2,1)S(1)}, bf16[32,4096]{1,0:T(8,128)(2,1)}, u32[]{:S(2)}, u32[]{:S(2)}) collective-permute-start(bf16[32,4096]{1,0:T(8,128)(2,1)S(1)} %get-tuple-element.430), channel_id=1, source_target_pairs={{0,288},{32,320},{64,352},{96,384},{128,416},{160,448},{192,480},{... | collective-permute-start | bytes 786440 | tf_op jit(solution)/shard_map/cond/branch_21_fun/ppermute | solution.py:23
  41.2 11.3 %collective-permute-start.123 = (bf16[32,4096]{1,0:T(8,128)(2,1)S(1)}, bf16[32,4096]{1,0:T(8,128)(2,1)}, u32[]{:S(2)}, u32[]{:S(2)}) collective-permute-start(bf16[32,4096]{1,0:T(8,128)(2,1)S(1)} %get-tuple-element.431), channel_id=1, source_target_pairs={{0,320},{32,352},{64,384},{96,416},{128,448},{160,480},{192,512},{... | collective-permute-start | bytes 786440 | tf_op jit(solution)/shard_map/cond/branch_21_fun/ppermute | solution.py:23
  52.4 0.0 collective-permute-done.121
  52.5 37.9 %collective-permute-done.122 = bf16[32,4096]{1,0:T(8,128)(2,1)} collective-permute-done((bf16[32,4096]{1,0:T(8,128)(2,1)S(1)}, bf16[32,4096]{1,0:T(8,128)(2,1)}, u32[]{:S(2)}, u32[]{:S(2)}) %collective-permute-start.122) | collective-permute-done | bytes 262176 | tf_op jit(solution)/shard_map/cond/branch_21_fun/ppermute | solution.py:23
  90.4 0.0 collective-permute-done.123
  90.4 1.5 fusion.5
  91.8 8.1 %collective-permute-start.145 = (bf16[32,4096]{1,0:T(8,128)(2,1)S(1)}, bf16[32,4096]{1,0:T(8,128)(2,1)S(1)}, u32[]{:S(2)}, u32[]{:S(2)}) collective-permute-start(bf16[32,4096]{1,0:T(8,128)(2,1)S(1)} %get-tuple-element.467), channel_id=1, source_target_pairs={{0,32},{32,64},{64,96},{96,128},{128,160},{160,192},{192,224},{224... | collective-permute-start | bytes 786440 | tf_op jit(solution)/shard_map/ppermute | solution.py:23
  100.0 0.1 broadcast_in_dim.7
  100.0 10.8 %all_to_all.6 = f32[8,1,4096]{2,1,0:T(1,128)S(1)} all-to-all(f32[8,1,4096]{2,1,0:T(1,128)S(1)} %broadcast_in_dim.7), channel_id=1, replica_groups={{0,1,8,9,16,17,24,25},{2,3,10,11,18,19,26,27},{4,5,12,13,20,21,28,29},{..., dimensions={0} | all-to-all | bytes 262144 | tf_op jit(solution)/shard_map/all_to_all | solution.py:154
  110.8 0.1 reduce_sum.39
  110.9 15.4 %collective-permute-start.147 = (f32[1,4096]{1,0:T(1,128)S(1)}, f32[1,4096]{1,0:T(1,128)S(1)}, u32[]{:S(2)}, u32[]{:S(2)}) collective-permute-start(f32[1,4096]{1,0:T(1,128)S(1)} %bitcast.29), channel_id=1, source_target_pairs={{0,2},{1,3},{2,4},{3,5},{4,6},{5,7},{6,0},{7,1},{8,10},{9,11},{10,... | collective-permute-start | bytes 49160 | tf_op jit(solution)/shard_map/ppermute | solution.py:167
  126.3 12.3 %collective-permute-start.148 = (f32[1,4096]{1,0:T(1,128)S(1)}, f32[1,4096]{1,0:T(1,128)S(1)}, u32[]{:S(2)}, u32[]{:S(2)}) collective-permute-start(f32[1,4096]{1,0:T(1,128)S(1)} %bitcast.30), channel_id=1, source_target_pairs={{0,4},{1,5},{2,6},{3,7},{4,0},{5,1},{6,2},{7,3},{8,12},{9,13},{10,... | collective-permute-start | bytes 49160 | tf_op jit(solution)/shard_map/ppermute | solution.py:167
  138.6 8.2 %collective-permute-start.149 = (f32[1,4096]{1,0:T(1,128)S(1)}, f32[1,4096]{1,0:T(1,128)S(1)}, u32[]{:S(2)}, u32[]{:S(2)}) collective-permute-start(f32[1,4096]{1,0:T(1,128)S(1)} %bitcast.31), channel_id=1, source_target_pairs={{0,6},{1,7},{2,0},{3,1},{4,2},{5,3},{6,4},{7,5},{8,14},{9,15},{10,... | collective-permute-start | bytes 49160 | tf_op jit(solution)/shard_map/ppermute | solution.py:167
  146.8 1.0 fusion.4
  147.9 1.9 %collective-permute-start.146 = (bf16[32,4096]{1,0:T(8,128)(2,1)S(1)}, bf16[32,4096]{1,0:T(8,128)(2,1)S(1)}, u32[]{:S(2)}, u32[]{:S(2)}) collective-permute-start(bf16[32,4096]{1,0:T(8,128)(2,1)S(1)} %fusion.4), channel_id=1, source_target_pairs={{0,32},{32,64},{64,96},{96,128},{128,160},{160,192},{192,224},{224... | collective-permute-start | bytes 786440 | tf_op jit(solution)/shard_map/ppermute | solution.py:23
  149.8 0.0 collective-permute-done.148
  149.8 2.3 %collective-permute-done.149 = f32[1,4096]{1,0:T(1,128)S(1)} collective-permute-done((f32[1,4096]{1,0:T(1,128)S(1)}, f32[1,4096]{1,0:T(1,128)S(1)}, u32[]{:S(2)}, u32[]{:S(2)}) %collective-permute-start.149) | collective-permute-done | bytes 16416 | tf_op jit(solution)/shard_map/ppermute | solution.py:167
  152.1 0.6 add_add_fusion
  152.7 12.2 %collective-permute-done.146 = bf16[32,4096]{1,0:T(8,128)(2,1)S(1)} collective-permute-done((bf16[32,4096]{1,0:T(8,128)(2,1)S(1)}, bf16[32,4096]{1,0:T(8,128)(2,1)S(1)}, u32[]{:S(2)}, u32[]{:S(2)}) %collective-permute-start.146) | collective-permute-done | bytes 262176 | tf_op jit(solution)/shard_map/ppermute | solution.py:23
  164.8 1.7 %fusion.9 = bf16[1,1,32,4096]{3,2,1,0:T(8,128)(2,1)} fusion(bf16[32,4096]{1,0:T(8,128)(2,1)} %get-tuple-element.477, bf16[32,4096]{1,0:T(8,128)(2,1)S(1)} %collective-permute-done.146, f32[4096]{0:T(1024)S(1)} %bitcast.28), kind=kLoop, calls=%fused_computation.15 | loop fusion | flops 655360 | bytes 802816 | tf_op jit(solution)/shard_map/broadcast_in_dim | solution.py:194
  (7 shorter events, 0.0 us)
Async XLA Ops:
  0.6 89.7 %copy-start.1 = (bf16[1,1,32,4096]{3,2,1,0:T(8,128)(2,1)S(1)}, bf16[1,1,32,4096]{3,2,1,0:T(8,128)(2,1)}, u32[]{:S(2)}) copy-start(bf16[1,1,32,4096]{3,2,1,0:T(8,128)(2,1)} %param.65) | copy-start | bytes 786436
  4.4 19.2 %collective-permute-start.42 = (bf16[34,32,128]{2,1,0:T(8,128)(2,1)S(1)}, bf16[34,32,128]{2,1,0:T(8,128)(2,1)}, u32[]{:S(2)}, u32[]{:S(2)}) collective-permute-start(bf16[34,32,128]{2,1,0:T(8,128)(2,1)S(1)} %get-tuple-element.350), channel_id=1, source_target_pairs={{0,768},{32,800},{64,832},{96,864},{128,896},{160,928},{192,960},{... | collective-permute-start | bytes 835592 | tf_op jit(solution)/shard_map/cond/branch_21_fun/ppermute | solution.py:23
  16.8 6.8 %collective-permute-start.43 = (bf16[1,4096]{1,0:T(2,128)(2,1)}, bf16[1,4096]{1,0:T(2,128)(2,1)}, u32[]{:S(2)}, u32[]{:S(2)}) collective-permute-start(bf16[1,4096]{1,0:T(2,128)(2,1)} %get-tuple-element.351), channel_id=1, source_target_pairs={{0,736},{32,768},{64,800},{96,832},{128,864},{160,896},{192,928},{... | collective-permute-start | bytes 24584 | tf_op jit(solution)/shard_map/cond/branch_21_fun/ppermute | solution.py:23
  23.6 1.6 copy-start
  25.2 65.2 %copy-start.2 = (bf16[1,3,1,32,4096]{4,3,2,1,0:T(8,128)(2,1)S(1)}, bf16[1,3,1,32,4096]{4,3,2,1,0:T(8,128)(2,1)}, u32[]{:S(2)}) copy-start(bf16[1,3,1,32,4096]{4,3,2,1,0:T(8,128)(2,1)} %param.71) | copy-start | bytes 2359300
  28.8 23.6 %collective-permute-start.121 = (bf16[32,4096]{1,0:T(8,128)(2,1)S(1)}, bf16[32,4096]{1,0:T(8,128)(2,1)}, u32[]{:S(2)}, u32[]{:S(2)}) collective-permute-start(bf16[32,4096]{1,0:T(8,128)(2,1)S(1)} %get-tuple-element.429), channel_id=1, source_target_pairs={{0,256},{32,288},{64,320},{96,352},{128,384},{160,416},{192,448},{... | collective-permute-start | bytes 786440 | tf_op jit(solution)/shard_map/cond/branch_21_fun/ppermute | solution.py:23
  35.4 54.9 %collective-permute-start.122 = (bf16[32,4096]{1,0:T(8,128)(2,1)S(1)}, bf16[32,4096]{1,0:T(8,128)(2,1)}, u32[]{:S(2)}, u32[]{:S(2)}) collective-permute-start(bf16[32,4096]{1,0:T(8,128)(2,1)S(1)} %get-tuple-element.430), channel_id=1, source_target_pairs={{0,288},{32,320},{64,352},{96,384},{128,416},{160,448},{192,480},{... | collective-permute-start | bytes 786440 | tf_op jit(solution)/shard_map/cond/branch_21_fun/ppermute | solution.py:23
  41.2 49.2 %collective-permute-start.123 = (bf16[32,4096]{1,0:T(8,128)(2,1)S(1)}, bf16[32,4096]{1,0:T(8,128)(2,1)}, u32[]{:S(2)}, u32[]{:S(2)}) collective-permute-start(bf16[32,4096]{1,0:T(8,128)(2,1)S(1)} %get-tuple-element.431), channel_id=1, source_target_pairs={{0,320},{32,352},{64,384},{96,416},{128,448},{160,480},{192,512},{... | collective-permute-start | bytes 786440 | tf_op jit(solution)/shard_map/cond/branch_21_fun/ppermute | solution.py:23
  91.8 55.0 %collective-permute-start.145 = (bf16[32,4096]{1,0:T(8,128)(2,1)S(1)}, bf16[32,4096]{1,0:T(8,128)(2,1)S(1)}, u32[]{:S(2)}, u32[]{:S(2)}) collective-permute-start(bf16[32,4096]{1,0:T(8,128)(2,1)S(1)} %get-tuple-element.467), channel_id=1, source_target_pairs={{0,32},{32,64},{64,96},{96,128},{128,160},{160,192},{192,224},{224... | collective-permute-start | bytes 786440 | tf_op jit(solution)/shard_map/ppermute | solution.py:23
  110.9 38.9 %collective-permute-start.147 = (f32[1,4096]{1,0:T(1,128)S(1)}, f32[1,4096]{1,0:T(1,128)S(1)}, u32[]{:S(2)}, u32[]{:S(2)}) collective-permute-start(f32[1,4096]{1,0:T(1,128)S(1)} %bitcast.29), channel_id=1, source_target_pairs={{0,2},{1,3},{2,4},{3,5},{4,6},{5,7},{6,0},{7,1},{8,10},{9,11},{10,... | collective-permute-start | bytes 49160 | tf_op jit(solution)/shard_map/ppermute | solution.py:167
  126.3 23.5 %collective-permute-start.148 = (f32[1,4096]{1,0:T(1,128)S(1)}, f32[1,4096]{1,0:T(1,128)S(1)}, u32[]{:S(2)}, u32[]{:S(2)}) collective-permute-start(f32[1,4096]{1,0:T(1,128)S(1)} %bitcast.30), channel_id=1, source_target_pairs={{0,4},{1,5},{2,6},{3,7},{4,0},{5,1},{6,2},{7,3},{8,12},{9,13},{10,... | collective-permute-start | bytes 49160 | tf_op jit(solution)/shard_map/ppermute | solution.py:167
  138.6 13.4 %collective-permute-start.149 = (f32[1,4096]{1,0:T(1,128)S(1)}, f32[1,4096]{1,0:T(1,128)S(1)}, u32[]{:S(2)}, u32[]{:S(2)}) collective-permute-start(f32[1,4096]{1,0:T(1,128)S(1)} %bitcast.31), channel_id=1, source_target_pairs={{0,6},{1,7},{2,0},{3,1},{4,2},{5,3},{6,4},{7,5},{8,14},{9,15},{10,... | collective-permute-start | bytes 49160 | tf_op jit(solution)/shard_map/ppermute | solution.py:167
  147.9 17.0 %collective-permute-start.146 = (bf16[32,4096]{1,0:T(8,128)(2,1)S(1)}, bf16[32,4096]{1,0:T(8,128)(2,1)S(1)}, u32[]{:S(2)}, u32[]{:S(2)}) collective-permute-start(bf16[32,4096]{1,0:T(8,128)(2,1)S(1)} %fusion.4), channel_id=1, source_target_pairs={{0,32},{32,64},{64,96},{96,128},{128,160},{160,192},{192,224},{224... | collective-permute-start | bytes 786440 | tf_op jit(solution)/shard_map/ppermute | solution.py:23

commit v3 on v2

--- a/solution.py
+++ b/solution.py
@@ -89,8 +89,12 @@
                 preferred_element_type=jnp.float32,
             ).astype(jnp.bfloat16)
             mixed = jnp.where(row_live, mixed.astype(jnp.float32), 0.0)
-            out_refs[t][:, h * HD : (h + 1) * HD] = mixed.astype(jnp.bfloat16)
-            if t + 1 < STEPS:
+            out_refs[t][:rows, h * HD : (h + 1) * HD] = mixed.astype(jnp.bfloat16)
+            if t + 1 == STEPS:
+                for j in range(per_head):
+                    b = h * per_head + j
+                    out_refs[t][rows:, b * LANES : (b + 1) * LANES] = source[b]
+            else:
                 for j in range(per_head):
                     b = h * per_head + j
                     if t == 0:
@@ -108,7 +112,10 @@
     keys, width = memory.shape[1:]
     return pl.pallas_call(
         steps_kernel,
-        out_shape=[jax.ShapeDtypeStruct((rows, width), jnp.bfloat16)] * STEPS,
+        out_shape=[
+            jax.ShapeDtypeStruct((rows * (1 + (t + 1 == STEPS)), width), jnp.bfloat16)
+            for t in range(STEPS)
+        ],
         in_specs=[SMEM, VMEM, VMEM, VMEM],
         out_specs=[VMEM] * STEPS,
         scratch_shapes=[
@@ -135,7 +142,8 @@
 
 
 def to_owner(offset, message, gain):
-    return shifted(message, "section", offset), shifted(gain, "section", offset - 1)
+    message = shifted(message, "section", offset)
+    return message, shifted(gain, "section", offset - 1)
 
 
 def from_owner(offset, *attended):
@@ -155,21 +163,19 @@
     )
 
 
-def from_run(row, step):
+def far_dp_sum(row):
     count = lax.axis_size("dp")
     runs = count // (ROWS_Y * CORES)
-
-    def target(source):
-        y, rest = divmod(source, runs * CORES)
-        run, core = divmod(rest, CORES)
-        return (y * runs + (run + step) % runs) * CORES + core
-
-    return lax.ppermute(row, "dp", [(s, target(s)) for s in range(count)])
+    groups = [
+        [(y * runs + run) * CORES + core for run in range(runs)]
+        for y in range(ROWS_Y)
+        for core in range(CORES)
+    ]
+    return lax.psum(row, "dp", axis_index_groups=groups)
 
 
 def per_device(states, memory, memory_len, decode_len, owner_map, section_gain, cotangent):
     sections = lax.axis_size("section")
-    runs = lax.axis_size("dp") // (ROWS_Y * CORES)
     state, gain = states[0, 0], section_gain
     offset_index = owner_map[0] - LEAST_OFFSET
 
@@ -178,20 +184,16 @@
     sent = attended_steps(message, gain_next, memory[0, 0], memory_len[0])
     sent = by_offset(offset_index, sections, from_owner, *sent)
 
+    rows = state.shape[0]
     total = jnp.zeros((1, state.shape[1]), jnp.float32)
     for t in range(STEPS):
         total = total + jnp.sum(
-            cotangent[0, t, 0].astype(jnp.float32) * sent[t].astype(jnp.float32),
+            cotangent[0, t, 0].astype(jnp.float32) * sent[t][:rows].astype(jnp.float32),
             axis=0,
             keepdims=True,
         )
-    total, state = lax.optimization_barrier((total, updated(state, gain, sent[0])))
-    state = shifted(state, "section", 1)
-    total = near_dp_sum(total)
-    arrived = [from_run(total, step) for step in range(1, runs)]
-    state = shifted(updated(state, gain, sent[1]), "section", 1)
-    state = updated(state, gain, sent[2])
-    return (state[None, None], sum(arrived, total))
+    state = updated(sent[-1][rows:], gain, sent[-1][:rows])
+    return (state[None, None], far_dp_sum(near_dp_sum(total)))
 
 
 def solution(mesh):

time: 167 us -> 172 us (1.030)
  the two profiles are of different devices: /device:TPU:1 before, /device:TPU:2 now
where the time goes in v3:
time: 172 us
  waiting for transfers between devices  70.3 us (41%)
  blocking collectives  58.7 us (34%)
  starting transfers between devices  30.8 us (18%)
  Pallas kernels  4.72 us (3%)
  other arithmetic  3 us (2%)
  between operations  2.6 us (2%)
    ppermute x5, waiting for transfers between devices, shifted(): return lax.ppermute(value, axis, pairs)  70.3 us
    psum x1, blocking collectives, far_dp_sum(): return lax.psum(row, 'dp', axis_index_groups=groups)  48.3 us
    ppermute x5, starting transfers between devices, shifted(): return lax.ppermute(value, axis, pairs)  30.8 us
    all_to_all x1, blocking collectives, near_dp_sum(): lax.all_to_all(copies, 'dp', 0, 0, axis_index_groups=groups)  10.4 us
    pallas_call x1, Pallas kernels, attended_steps(): pl.pallas_call(steps_kernel, out_shape=[jax.ShapeDtypeStruct((rows * (1 +...  3.7 us
  transfers between devices with their start and end apart: 5, of which 3 were waited for; matrix products, arithmetic and copies ran while one was open for 0% of the time, Pallas kernels for 0%

profile of v3, /device:TPU:2, one launch (start us, length us, event | category | flops | bytes accessed | tf_op | source)
XLA Modules:
  0.0 171.8 jit_solution(14013763873058358231)
XLA Ops:
  1.3 0.7 mul.29
  2.0 1.0 pack.1
  4.3 22.6 %conditional.4 = (bf16[34,32,128]{2,1,0:T(8,128)(2,1)}, bf16[1,4096]{1,0:T(2,128)(2,1)}) conditional(s32[]{:T(128)} %bitcast, (bf16[34,32,128]{2,1,0:T(8,128)(2,1)S(1)}, bf16[1,4096]{1,0:T(2,128)(2,1)}) %tuple.416, (bf16[34,32,128]{2,1,0:T(8,128)(2,1)S(1)}, bf16[1,4096]{1,0:T(2,128)(2,1)}) %tuple.416, ...), branch_computations={%region_0.0_spmd, %region_1.0_spmd, %region_2.0_spmd, %region_3.0_... | conditional | bytes 1146976 | solution.py:137
  4.4 12.0 %collective-permute-start.38 = (bf16[34,32,128]{2,1,0:T(8,128)(2,1)S(1)}, bf16[34,32,128]{2,1,0:T(8,128)(2,1)}, u32[]{:S(2)}, u32[]{:S(2)}) collective-permute-start(bf16[34,32,128]{2,1,0:T(8,128)(2,1)S(1)} %get-tuple-element.342), channel_id=1, source_target_pairs={{0,704},{32,736},{64,768},{96,800},{128,832},{160,864},{192,896},{... | collective-permute-start | bytes 835592 | tf_op jit(solution)/shard_map/cond/branch_19_fun/ppermute | solution.py:23
  16.4 1.9 %collective-permute-start.39 = (bf16[1,4096]{1,0:T(2,128)(2,1)}, bf16[1,4096]{1,0:T(2,128)(2,1)}, u32[]{:S(2)}, u32[]{:S(2)}) collective-permute-start(bf16[1,4096]{1,0:T(2,128)(2,1)} %get-tuple-element.343), channel_id=1, source_target_pairs={{0,672},{32,704},{64,736},{96,768},{128,800},{160,832},{192,864},{... | collective-permute-start | bytes 24584 | tf_op jit(solution)/shard_map/cond/branch_19_fun/ppermute | solution.py:23
  18.3 8.6 %collective-permute-done.39 = bf16[1,4096]{1,0:T(2,128)(2,1)} collective-permute-done((bf16[1,4096]{1,0:T(2,128)(2,1)}, bf16[1,4096]{1,0:T(2,128)(2,1)}, u32[]{:S(2)}, u32[]{:S(2)}) %collective-permute-start.39) | collective-permute-done | bytes 8224 | tf_op jit(solution)/shard_map/cond/branch_19_fun/ppermute | solution.py:23
  26.9 0.0 collective-permute-done.38
  26.9 0.0 copy-start
  26.9 1.6 copy-done
  28.5 0.0 copy-start.1
  28.5 3.7 %steps.1 = (bf16[32,4096]{1,0:T(8,128)(2,1)S(1)}, bf16[32,4096]{1,0:T(8,128)(2,1)S(1)}, bf16[64,4096]{1,0:T(8,128)(2,1)S(1)}) custom-call(s32[1]{0:T(128)} %bitcast.19.key_len_ref, bf16[34,32,128]{2,1,0:T(8,128)(2,1)} %get-tuple-element.459.message_ref, bf16[1,4096]{1,0:T(2,128)(2,1)} %get-tuple-element.460.gain_next_ref, bf16[2,128,4096]{2,1,0:T(8,128)(2,1)S(1)} %bitcast.21), custom_call_target="tpu_custom_call" | custom-call | tf_op jit(solution)/shard_map/steps/pallas_call | solution.py:113
  32.2 78.6 %conditional.6 = (bf16[64,4096]{1,0:T(8,128)(2,1)}, bf16[32,4096]{1,0:T(8,128)(2,1)}, bf16[32,4096]{1,0:T(8,128)(2,1)}) conditional(s32[]{:T(128)} %bitcast, (bf16[64,4096]{1,0:T(8,128)(2,1)S(1)}, bf16[32,4096]{1,0:T(8,128)(2,1)S(1)}, bf16[32,4096]{1,0:T(8,128)(2,1)S(1)}) %tuple.417, (bf16[64,4096]{1,0:T(8,128)(2,1)S(1)}, ...), branch_computations={%region_29.0_spmd, %region_30.0_spmd, %region_31.0_spmd, %region_3... | conditional | bytes 4194448
  32.2 6.8 %collective-permute-start.115 = (bf16[64,4096]{1,0:T(8,128)(2,1)S(1)}, bf16[64,4096]{1,0:T(8,128)(2,1)}, u32[]{:S(2)}, u32[]{:S(2)}) collective-permute-start(bf16[64,4096]{1,0:T(8,128)(2,1)S(1)} %get-tuple-element.419), channel_id=1, source_target_pairs={{0,384},{32,416},{64,448},{96,480},{128,512},{160,544},{192,576},{... | collective-permute-start | bytes 1572872 | tf_op jit(solution)/shard_map/cond/branch_19_fun/ppermute | solution.py:23
  39.0 8.2 %collective-permute-start.116 = (bf16[32,4096]{1,0:T(8,128)(2,1)S(1)}, bf16[32,4096]{1,0:T(8,128)(2,1)}, u32[]{:S(2)}, u32[]{:S(2)}) collective-permute-start(bf16[32,4096]{1,0:T(8,128)(2,1)S(1)} %get-tuple-element.420), channel_id=1, source_target_pairs={{0,320},{32,352},{64,384},{96,416},{128,448},{160,480},{192,512},{... | collective-permute-start | bytes 786440 | tf_op jit(solution)/shard_map/cond/branch_19_fun/ppermute | solution.py:23
  47.2 1.9 %collective-permute-start.117 = (bf16[32,4096]{1,0:T(8,128)(2,1)S(1)}, bf16[32,4096]{1,0:T(8,128)(2,1)}, u32[]{:S(2)}, u32[]{:S(2)}) collective-permute-start(bf16[32,4096]{1,0:T(8,128)(2,1)S(1)} %get-tuple-element.421), channel_id=1, source_target_pairs={{0,352},{32,384},{64,416},{96,448},{128,480},{160,512},{192,544},{... | collective-permute-start | bytes 786440 | tf_op jit(solution)/shard_map/cond/branch_19_fun/ppermute | solution.py:23
  49.1 59.7 %collective-permute-done.116 = bf16[32,4096]{1,0:T(8,128)(2,1)} collective-permute-done((bf16[32,4096]{1,0:T(8,128)(2,1)S(1)}, bf16[32,4096]{1,0:T(8,128)(2,1)}, u32[]{:S(2)}, u32[]{:S(2)}) %collective-permute-start.116) | collective-permute-done | bytes 262176 | tf_op jit(solution)/shard_map/cond/branch_19_fun/ppermute | solution.py:23
  108.8 2.0 %collective-permute-done.117 = bf16[32,4096]{1,0:T(8,128)(2,1)} collective-permute-done((bf16[32,4096]{1,0:T(8,128)(2,1)S(1)}, bf16[32,4096]{1,0:T(8,128)(2,1)}, u32[]{:S(2)}, u32[]{:S(2)}) %collective-permute-start.117) | collective-permute-done | bytes 262176 | tf_op jit(solution)/shard_map/cond/branch_19_fun/ppermute | solution.py:23
  110.8 0.0 collective-permute-done.115
  110.8 0.0 copy-done.1
  110.8 2.2 %fusion.3 = (f32[4096]{0:T(1024)S(1)}, f32[4096]{0:T(1024)S(1)}, f32[4096]{0:T(1024)S(1)}, bf16[1,1,32,4096]{3,2,1,0:T(8,128)(2,1)}) fusion(bf16[32,4096]{1,0:T(8,128)(2,1)} %get-tuple-element.473, bf16[1,3,1,32,4096]{4,3,2,1,0:T(8,128)(2,1)S(1)} %copy-done.1, bf16[32,4096]{1,0:T(8,128)(2,1)} %get-tuple-element.472, bf16[64,4096]{1,0:T(8,128)(2,1)} %get-tuple-element.464, ...), kind=kLoop, calls=%fused_computation.6 | loop fusion | flops 2084864 | bytes 2162688 | tf_op jit(solution)/shard_map/reduce_sum | solution.py:190
  113.0 0.1 broadcast_in_dim.7
  113.1 10.4 %all_to_all.6 = f32[8,1,4096]{2,1,0:T(1,128)S(1)} all-to-all(f32[8,1,4096]{2,1,0:T(1,128)S(1)} %broadcast_in_dim.7), channel_id=1, replica_groups={{0,1,8,9,16,17,24,25},{2,3,10,11,18,19,26,27},{4,5,12,13,20,21,28,29},{..., dimensions={0} | all-to-all | bytes 262144 | tf_op jit(solution)/shard_map/all_to_all | solution.py:162
  123.5 0.1 reduce_sum.39
  123.6 48.3 %psum.7 = f32[1,4096]{1,0:T(1,128)} all-reduce(f32[1,4096]{1,0:T(1,128)S(1)} %bitcast.24), channel_id=1, replica_groups={{0,2,4,6},{1,3,5,7},{8,10,12,14},{9,11,13,15},{16,18,20,22},{17,19,21,2..., use_global_device_ids=true, to_apply=%region_62.0 | all-reduce | flops 4096 | bytes 32768 | tf_op jit(solution)/shard_map/psum | solution.py:174
  (1 shorter events, 0.0 us)
Async XLA Ops:
  4.4 22.5 %collective-permute-start.38 = (bf16[34,32,128]{2,1,0:T(8,128)(2,1)S(1)}, bf16[34,32,128]{2,1,0:T(8,128)(2,1)}, u32[]{:S(2)}, u32[]{:S(2)}) collective-permute-start(bf16[34,32,128]{2,1,0:T(8,128)(2,1)S(1)} %get-tuple-element.342), channel_id=1, source_target_pairs={{0,704},{32,736},{64,768},{96,800},{128,832},{160,864},{192,896},{... | collective-permute-start | bytes 835592 | tf_op jit(solution)/shard_map/cond/branch_19_fun/ppermute | solution.py:23
  16.4 10.5 %collective-permute-start.39 = (bf16[1,4096]{1,0:T(2,128)(2,1)}, bf16[1,4096]{1,0:T(2,128)(2,1)}, u32[]{:S(2)}, u32[]{:S(2)}) collective-permute-start(bf16[1,4096]{1,0:T(2,128)(2,1)} %get-tuple-element.343), channel_id=1, source_target_pairs={{0,672},{32,704},{64,736},{96,768},{128,800},{160,832},{192,864},{... | collective-permute-start | bytes 24584 | tf_op jit(solution)/shard_map/cond/branch_19_fun/ppermute | solution.py:23
  26.9 1.6 copy-start
  28.5 82.4 %copy-start.1 = (bf16[1,3,1,32,4096]{4,3,2,1,0:T(8,128)(2,1)S(1)}, bf16[1,3,1,32,4096]{4,3,2,1,0:T(8,128)(2,1)}, u32[]{:S(2)}) copy-start(bf16[1,3,1,32,4096]{4,3,2,1,0:T(8,128)(2,1)} %param.71) | copy-start | bytes 2359300
  32.2 78.6 %collective-permute-start.115 = (bf16[64,4096]{1,0:T(8,128)(2,1)S(1)}, bf16[64,4096]{1,0:T(8,128)(2,1)}, u32[]{:S(2)}, u32[]{:S(2)}) collective-permute-start(bf16[64,4096]{1,0:T(8,128)(2,1)S(1)} %get-tuple-element.419), channel_id=1, source_target_pairs={{0,384},{32,416},{64,448},{96,480},{128,512},{160,544},{192,576},{... | collective-permute-start | bytes 1572872 | tf_op jit(solution)/shard_map/cond/branch_19_fun/ppermute | solution.py:23
  39.0 69.8 %collective-permute-start.116 = (bf16[32,4096]{1,0:T(8,128)(2,1)S(1)}, bf16[32,4096]{1,0:T(8,128)(2,1)}, u32[]{:S(2)}, u32[]{:S(2)}) collective-permute-start(bf16[32,4096]{1,0:T(8,128)(2,1)S(1)} %get-tuple-element.420), channel_id=1, source_target_pairs={{0,320},{32,352},{64,384},{96,416},{128,448},{160,480},{192,512},{... | collective-permute-start | bytes 786440 | tf_op jit(solution)/shard_map/cond/branch_19_fun/ppermute | solution.py:23
  47.2 63.7 %collective-permute-start.117 = (bf16[32,4096]{1,0:T(8,128)(2,1)S(1)}, bf16[32,4096]{1,0:T(8,128)(2,1)}, u32[]{:S(2)}, u32[]{:S(2)}) collective-permute-start(bf16[32,4096]{1,0:T(8,128)(2,1)S(1)} %get-tuple-element.421), channel_id=1, source_target_pairs={{0,352},{32,384},{64,416},{96,448},{128,480},{160,512},{192,544},{... | collective-permute-start | bytes 786440 | tf_op jit(solution)/shard_map/cond/branch_19_fun/ppermute | solution.py:23

commit v4 on v3

--- a/solution.py
+++ b/solution.py
@@ -89,12 +89,8 @@
                 preferred_element_type=jnp.float32,
             ).astype(jnp.bfloat16)
             mixed = jnp.where(row_live, mixed.astype(jnp.float32), 0.0)
-            out_refs[t][:rows, h * HD : (h + 1) * HD] = mixed.astype(jnp.bfloat16)
-            if t + 1 == STEPS:
-                for j in range(per_head):
-                    b = h * per_head + j
-                    out_refs[t][rows:, b * LANES : (b + 1) * LANES] = source[b]
-            else:
+            out_refs[t][:, h * HD : (h + 1) * HD] = mixed.astype(jnp.bfloat16)
+            if t + 1 < STEPS:
                 for j in range(per_head):
                     b = h * per_head + j
                     if t == 0:
@@ -112,10 +108,7 @@
     keys, width = memory.shape[1:]
     return pl.pallas_call(
         steps_kernel,
-        out_shape=[
-            jax.ShapeDtypeStruct((rows * (1 + (t + 1 == STEPS)), width), jnp.bfloat16)
-            for t in range(STEPS)
-        ],
+        out_shape=[jax.ShapeDtypeStruct((rows, width), jnp.bfloat16)] * STEPS,
         in_specs=[SMEM, VMEM, VMEM, VMEM],
         out_specs=[VMEM] * STEPS,
         scratch_shapes=[
@@ -143,7 +136,7 @@
 
 def to_owner(offset, message, gain):
     message = shifted(message, "section", offset)
-    return message, shifted(gain, "section", offset - 1)
+    return message, shifted(gain, "section", offset - 1), shifted(gain, "section", 1)
 
 
 def from_owner(offset, *attended):
@@ -180,20 +173,24 @@
     offset_index = owner_map[0] - LEAST_OFFSET
 
     message = packed(state, gain, decode_len[0])
-    message, gain_next = by_offset(offset_index, sections, to_owner, message, gain)
+    message, gain_next, gain_before = by_offset(offset_index, sections, to_owner, message, gain)
     sent = attended_steps(message, gain_next, memory[0, 0], memory_len[0])
     sent = by_offset(offset_index, sections, from_owner, *sent)
 
-    rows = state.shape[0]
     total = jnp.zeros((1, state.shape[1]), jnp.float32)
     for t in range(STEPS):
         total = total + jnp.sum(
-            cotangent[0, t, 0].astype(jnp.float32) * sent[t][:rows].astype(jnp.float32),
+            cotangent[0, t, 0].astype(jnp.float32) * sent[t].astype(jnp.float32),
             axis=0,
             keepdims=True,
         )
-    state = updated(sent[-1][rows:], gain, sent[-1][:rows])
-    return (state[None, None], far_dp_sum(near_dp_sum(total)))
+    state = updated(state, gain, sent[0])
+    total, state, middle = lax.optimization_barrier((near_dp_sum(total), state, sent[1]))
+    state = shifted(state, "section", 2)
+    middle = shifted(middle, "section", 1)
+    total = far_dp_sum(total)
+    state = updated(updated(state, gain_before, middle), gain, sent[2])
+    return (state[None, None], total)
 
 
 def solution(mesh):

time: 172 us -> 149 us (0.87)
  the two profiles are of different devices: /device:TPU:2 before, /device:TPU:230 now
where the time goes in v4:
time: 149 us
  blocking collectives  62.3 us (42%)
  starting transfers between devices  39.2 us (26%)
  waiting for transfers between devices  32.1 us (22%)
  other arithmetic  4.75 us (3%)
  Pallas kernels  4.57 us (3%)
  between operations  2.65 us (2%)
  local copies, waits for them, and re-layouts  2.62 us (2%)
    psum x1, blocking collectives, far_dp_sum(): return lax.psum(row, 'dp', axis_index_groups=groups)  51.4 us
    ppermute x8, starting transfers between devices, shifted(): return lax.ppermute(value, axis, pairs)  39.2 us
    ppermute x8, waiting for transfers between devices, shifted(): return lax.ppermute(value, axis, pairs)  32.1 us
    all_to_all x1, blocking collectives, near_dp_sum(): lax.all_to_all(copies, 'dp', 0, 0, axis_index_groups=groups)  10.9 us
    pallas_call x1, Pallas kernels, attended_steps(): pl.pallas_call(steps_kernel, out_shape=[jax.ShapeDtypeStruct((rows, width...  3.56 us
  transfers between devices with their start and end apart: 8, of which 5 were waited for; matrix products, arithmetic and copies ran while one was open for 1% of the time, Pallas kernels for 0%

profile of v4, /device:TPU:230, one launch (start us, length us, event | category | flops | bytes accessed | tf_op | source)
XLA Modules:
  0.0 148.5 jit_solution(12426167963587063672)
XLA Ops:
  1.3 0.7 mul.53
  2.0 1.0 pack.1
  4.3 23.0 %conditional.4 = (bf16[34,32,128]{2,1,0:T(8,128)(2,1)}, bf16[1,4096]{1,0:T(2,128)(2,1)}, bf16[1,4096]{1,0:T(2,128)(2,1)}) conditional(s32[]{:T(128)} %bitcast.1, (bf16[34,32,128]{2,1,0:T(8,128)(2,1)S(1)}, bf16[1,4096]{1,0:T(2,128)(2,1)}) %tuple.475, (bf16[34,32,128]{2,1,0:T(8,128)(2,1)S(1)}, ...), branch_computations={%region_0.0_spmd, %region_1.0_spmd, %region_2.0_spmd, %region_3.0_... | conditional | bytes 1179792 | solution.py:130
  4.4 1.9 %collective-permute-start.66 = (bf16[34,32,128]{2,1,0:T(8,128)(2,1)S(1)}, bf16[34,32,128]{2,1,0:T(8,128)(2,1)}, u32[]{:S(2)}, u32[]{:S(2)}) collective-permute-start(bf16[34,32,128]{2,1,0:T(8,128)(2,1)S(1)} %get-tuple-element.354), channel_id=1, source_target_pairs={{0,800},{32,832},{64,864},{96,896},{128,928},{160,960},{192,992},{... | collective-permute-start | bytes 835592 | tf_op jit(solution)/shard_map/cond/branch_22_fun/ppermute | solution.py:23
  6.3 1.9 %collective-permute-start.67 = (bf16[1,4096]{1,0:T(2,128)(2,1)}, bf16[1,4096]{1,0:T(2,128)(2,1)}, u32[]{:S(2)}, u32[]{:S(2)}) collective-permute-start(bf16[1,4096]{1,0:T(2,128)(2,1)} %get-tuple-element.355), channel_id=1, source_target_pairs={{0,768},{32,800},{64,832},{96,864},{128,896},{160,928},{192,960},{... | collective-permute-start | bytes 24584 | tf_op jit(solution)/shard_map/cond/branch_22_fun/ppermute | solution.py:23
  8.2 11.8 %collective-permute-start.68 = (bf16[1,4096]{1,0:T(2,128)(2,1)}, bf16[1,4096]{1,0:T(2,128)(2,1)}, u32[]{:S(2)}, u32[]{:S(2)}) collective-permute-start(bf16[1,4096]{1,0:T(2,128)(2,1)} %get-tuple-element.355), channel_id=1, source_target_pairs={{0,32},{32,64},{64,96},{96,128},{128,160},{160,192},{192,224},{224... | collective-permute-start | bytes 24584 | tf_op jit(solution)/shard_map/cond/branch_22_fun/ppermute | solution.py:23
  20.1 2.0 %collective-permute-done.67 = bf16[1,4096]{1,0:T(2,128)(2,1)} collective-permute-done((bf16[1,4096]{1,0:T(2,128)(2,1)}, bf16[1,4096]{1,0:T(2,128)(2,1)}, u32[]{:S(2)}, u32[]{:S(2)}) %collective-permute-start.67) | collective-permute-done | bytes 8224 | tf_op jit(solution)/shard_map/cond/branch_22_fun/ppermute | solution.py:23
  22.1 0.0 collective-permute-done.68
  22.1 5.2 %collective-permute-done.66 = bf16[34,32,128]{2,1,0:T(8,128)(2,1)} collective-permute-done((bf16[34,32,128]{2,1,0:T(8,128)(2,1)S(1)}, bf16[34,32,128]{2,1,0:T(8,128)(2,1)}, u32[]{:S(2)}, u32[]{:S(2)}) %collective-permute-start.66) | collective-permute-done | bytes 278560 | tf_op jit(solution)/shard_map/cond/branch_22_fun/ppermute | solution.py:23
  27.3 1.6 %copy-done = bf16[1,1,2,128,4096]{4,3,2,1,0:T(8,128)(2,1)S(1)} copy-done((bf16[1,1,2,128,4096]{4,3,2,1,0:T(8,128)(2,1)S(1)}, bf16[1,1,2,128,4096]{4,3,2,1,0:T(8,128)(2,1)}, u32[]{:S(2)}) %copy-start) | copy-done | bytes 2097176
  28.9 3.6 %steps.1 = (bf16[32,4096]{1,0:T(8,128)(2,1)S(1)}, bf16[32,4096]{1,0:T(8,128)(2,1)S(1)}, bf16[32,4096]{1,0:T(8,128)(2,1)S(1)}) custom-call(s32[1]{0:T(128)} %bitcast.21.key_len_ref, bf16[34,32,128]{2,1,0:T(8,128)(2,1)} %get-tuple-element.470.message_ref, bf16[1,4096]{1,0:T(2,128)(2,1)} %get-tuple-element.471.gain_next_ref, bf16[2,128,4096]{2,1,0:T(8,128)(2,1)S(1)} %bitcast.23), custom_call_target="tpu_custom_call" | custom-call | tf_op jit(solution)/shard_map/steps/pallas_call | solution.py:109
  32.5 0.0 copy-start.1
  32.5 0.0 copy-start.2
  32.5 34.0 %conditional.6 = (bf16[32,4096]{1,0:T(8,128)(2,1)}, bf16[32,4096]{1,0:T(8,128)(2,1)}, bf16[32,4096]{1,0:T(8,128)(2,1)S(1)}, bf16[32,4096]{1,0:T(8,128)(2,1)}) conditional(s32[]{:T(128)} %bitcast.1, (bf16[32,4096]{1,0:T(8,128)(2,1)S(1)}, bf16[32,4096]{1,0:T(8,128)(2,1)S(1)}, ...), branch_computations={%region_29.0_spmd, %region_30.0_spmd, %region_31.0_spmd, %region_3... | conditional | bytes 3670168
  32.7 2.1 %collective-permute-start.153 = (bf16[32,4096]{1,0:T(8,128)(2,1)S(1)}, bf16[32,4096]{1,0:T(8,128)(2,1)}, u32[]{:S(2)}, u32[]{:S(2)}) collective-permute-start(bf16[32,4096]{1,0:T(8,128)(2,1)S(1)} %get-tuple-element.434), channel_id=1, source_target_pairs={{0,256},{32,288},{64,320},{96,352},{128,384},{160,416},{192,448},{... | collective-permute-start | bytes 786440 | tf_op jit(solution)/shard_map/cond/branch_22_fun/ppermute | solution.py:23
  34.8 1.9 %collective-permute-start.154 = (bf16[32,4096]{1,0:T(8,128)(2,1)S(1)}, bf16[32,4096]{1,0:T(8,128)(2,1)}, u32[]{:S(2)}, u32[]{:S(2)}) collective-permute-start(bf16[32,4096]{1,0:T(8,128)(2,1)S(1)} %get-tuple-element.435), channel_id=1, source_target_pairs={{0,224},{32,256},{64,288},{96,320},{128,352},{160,384},{192,416},{... | collective-permute-start | bytes 786440 | tf_op jit(solution)/shard_map/cond/branch_22_fun/ppermute | solution.py:23
  36.7 4.0 %collective-permute-start.155 = (bf16[32,4096]{1,0:T(8,128)(2,1)S(1)}, bf16[32,4096]{1,0:T(8,128)(2,1)}, u32[]{:S(2)}, u32[]{:S(2)}) collective-permute-start(bf16[32,4096]{1,0:T(8,128)(2,1)S(1)} %get-tuple-element.436), channel_id=1, source_target_pairs={{0,288},{32,320},{64,352},{96,384},{128,416},{160,448},{192,480},{... | collective-permute-start | bytes 786440 | tf_op jit(solution)/shard_map/cond/branch_22_fun/ppermute | solution.py:23
  40.8 8.5 %collective-permute-done.153 = bf16[32,4096]{1,0:T(8,128)(2,1)} collective-permute-done((bf16[32,4096]{1,0:T(8,128)(2,1)S(1)}, bf16[32,4096]{1,0:T(8,128)(2,1)}, u32[]{:S(2)}, u32[]{:S(2)}) %collective-permute-start.153) | collective-permute-done | bytes 262176 | tf_op jit(solution)/shard_map/cond/branch_22_fun/ppermute | solution.py:23
  49.3 1.0 copy.188
  50.2 0.7 collective-permute-done.154
  50.9 15.6 %collective-permute-done.155 = bf16[32,4096]{1,0:T(8,128)(2,1)} collective-permute-done((bf16[32,4096]{1,0:T(8,128)(2,1)S(1)}, bf16[32,4096]{1,0:T(8,128)(2,1)}, u32[]{:S(2)}, u32[]{:S(2)}) %collective-permute-start.155) | collective-permute-done | bytes 262176 | tf_op jit(solution)/shard_map/cond/branch_22_fun/ppermute | solution.py:23
  66.5 1.4 fusion.6
  67.9 0.1 broadcast_in_dim.6
  68.0 10.9 %all_to_all.6 = f32[8,1,4096]{2,1,0:T(1,128)S(1)} all-to-all(f32[8,1,4096]{2,1,0:T(1,128)S(1)} %broadcast_in_dim.6), channel_id=1, replica_groups={{0,1,8,9,16,17,24,25},{2,3,10,11,18,19,26,27},{4,5,12,13,20,21,28,29},{..., dimensions={0} | all-to-all | bytes 262144 | tf_op jit(solution)/shard_map/all_to_all | solution.py:155
  78.9 0.1 reduce_sum.39
  79.0 8.4 %collective-permute-start.174 = (bf16[32,4096]{1,0:T(8,128)(2,1)S(1)}, bf16[32,4096]{1,0:T(8,128)(2,1)S(1)}, u32[]{:S(2)}, u32[]{:S(2)}) collective-permute-start(bf16[32,4096]{1,0:T(8,128)(2,1)S(1)} %get-tuple-element.479), channel_id=1, source_target_pairs={{0,64},{32,96},{64,128},{96,160},{128,192},{160,224},{192,256},{22... | collective-permute-start | bytes 786440 | tf_op jit(solution)/shard_map/ppermute | solution.py:23
  87.5 7.0 %collective-permute-start.175 = (bf16[32,4096]{1,0:T(8,128)(2,1)}, bf16[32,4096]{1,0:T(8,128)(2,1)S(1)}, u32[]{:S(2)}, u32[]{:S(2)}) collective-permute-start(bf16[32,4096]{1,0:T(8,128)(2,1)} %get-tuple-element.481), channel_id=1, source_target_pairs={{0,32},{32,64},{64,96},{96,128},{128,160},{160,192},{192,224},{224... | collective-permute-start | bytes 786440 | tf_op jit(solution)/shard_map/ppermute | solution.py:23
  94.5 0.7 mul.54
  95.3 51.4 %psum.7 = f32[1,4096]{1,0:T(1,128)} all-reduce(f32[1,4096]{1,0:T(1,128)S(1)} %bitcast.28), channel_id=1, replica_groups={{0,2,4,6},{1,3,5,7},{8,10,12,14},{9,11,13,15},{16,18,20,22},{17,19,21,2..., use_global_device_ids=true, to_apply=%region_62.0 | all-reduce | flops 4096 | bytes 32768 | tf_op jit(solution)/shard_map/psum | solution.py:167
  146.7 0.0 collective-permute-done.174
  146.7 0.0 collective-permute-done.175
  146.7 1.8 %fusion.7 = bf16[1,1,32,4096]{3,2,1,0:T(8,128)(2,1)} fusion(bf16[32,4096]{1,0:T(8,128)(2,1)} %get-tuple-element.492, bf16[32,4096]{1,0:T(8,128)(2,1)S(1)} %collective-permute-done.175, bf16[32,4096]{1,0:T(8,128)(2,1)S(1)} %collective-permute-done.174, f32[4096]{0:T(1024)S(1)} %bitcast.27, f32[4096]{0:T(1024)S(1)} %bitcast.26), kind=kLoop, calls=%fused_computation.13 | loop fusion | flops 1310720 | bytes 1081344 | tf_op jit(solution)/shard_map/broadcast_in_dim | solution.py:193
  (4 shorter events, 0.0 us)
Async XLA Ops:
  4.4 23.0 %collective-permute-start.66 = (bf16[34,32,128]{2,1,0:T(8,128)(2,1)S(1)}, bf16[34,32,128]{2,1,0:T(8,128)(2,1)}, u32[]{:S(2)}, u32[]{:S(2)}) collective-permute-start(bf16[34,32,128]{2,1,0:T(8,128)(2,1)S(1)} %get-tuple-element.354), channel_id=1, source_target_pairs={{0,800},{32,832},{64,864},{96,896},{128,928},{160,960},{192,992},{... | collective-permute-start | bytes 835592 | tf_op jit(solution)/shard_map/cond/branch_22_fun/ppermute | solution.py:23
  6.3 15.8 %collective-permute-start.67 = (bf16[1,4096]{1,0:T(2,128)(2,1)}, bf16[1,4096]{1,0:T(2,128)(2,1)}, u32[]{:S(2)}, u32[]{:S(2)}) collective-permute-start(bf16[1,4096]{1,0:T(2,128)(2,1)} %get-tuple-element.355), channel_id=1, source_target_pairs={{0,768},{32,800},{64,832},{96,864},{128,896},{160,928},{192,960},{... | collective-permute-start | bytes 24584 | tf_op jit(solution)/shard_map/cond/branch_22_fun/ppermute | solution.py:23
  8.2 13.8 %collective-permute-start.68 = (bf16[1,4096]{1,0:T(2,128)(2,1)}, bf16[1,4096]{1,0:T(2,128)(2,1)}, u32[]{:S(2)}, u32[]{:S(2)}) collective-permute-start(bf16[1,4096]{1,0:T(2,128)(2,1)} %get-tuple-element.355), channel_id=1, source_target_pairs={{0,32},{32,64},{64,96},{96,128},{128,160},{160,192},{192,224},{224... | collective-permute-start | bytes 24584 | tf_op jit(solution)/shard_map/cond/branch_22_fun/ppermute | solution.py:23
  27.3 1.6 %copy-start = (bf16[1,1,2,128,4096]{4,3,2,1,0:T(8,128)(2,1)S(1)}, bf16[1,1,2,128,4096]{4,3,2,1,0:T(8,128)(2,1)}, u32[]{:S(2)}) copy-start(bf16[1,1,2,128,4096]{4,3,2,1,0:T(8,128)(2,1)} %param.66) | copy-start | bytes 6291460
  32.5 34.1 %copy-start.1 = (bf16[1,1,32,4096]{3,2,1,0:T(8,128)(2,1)S(1)}, bf16[1,1,32,4096]{3,2,1,0:T(8,128)(2,1)}, u32[]{:S(2)}) copy-start(bf16[1,1,32,4096]{3,2,1,0:T(8,128)(2,1)} %param.65) | copy-start | bytes 786436
  32.5 34.1 %copy-start.2 = (bf16[1,3,1,32,4096]{4,3,2,1,0:T(8,128)(2,1)S(1)}, bf16[1,3,1,32,4096]{4,3,2,1,0:T(8,128)(2,1)}, u32[]{:S(2)}) copy-start(bf16[1,3,1,32,4096]{4,3,2,1,0:T(8,128)(2,1)} %param.71) | copy-start | bytes 2359300
  32.7 16.5 %collective-permute-start.153 = (bf16[32,4096]{1,0:T(8,128)(2,1)S(1)}, bf16[32,4096]{1,0:T(8,128)(2,1)}, u32[]{:S(2)}, u32[]{:S(2)}) collective-permute-start(bf16[32,4096]{1,0:T(8,128)(2,1)S(1)} %get-tuple-element.434), channel_id=1, source_target_pairs={{0,256},{32,288},{64,320},{96,352},{128,384},{160,416},{192,448},{... | collective-permute-start | bytes 786440 | tf_op jit(solution)/shard_map/cond/branch_22_fun/ppermute | solution.py:23
  34.8 16.1 %collective-permute-start.154 = (bf16[32,4096]{1,0:T(8,128)(2,1)S(1)}, bf16[32,4096]{1,0:T(8,128)(2,1)}, u32[]{:S(2)}, u32[]{:S(2)}) collective-permute-start(bf16[32,4096]{1,0:T(8,128)(2,1)S(1)} %get-tuple-element.435), channel_id=1, source_target_pairs={{0,224},{32,256},{64,288},{96,320},{128,352},{160,384},{192,416},{... | collective-permute-start | bytes 786440 | tf_op jit(solution)/shard_map/cond/branch_22_fun/ppermute | solution.py:23
  36.7 29.8 %collective-permute-start.155 = (bf16[32,4096]{1,0:T(8,128)(2,1)S(1)}, bf16[32,4096]{1,0:T(8,128)(2,1)}, u32[]{:S(2)}, u32[]{:S(2)}) collective-permute-start(bf16[32,4096]{1,0:T(8,128)(2,1)S(1)} %get-tuple-element.436), channel_id=1, source_target_pairs={{0,288},{32,320},{64,352},{96,384},{128,416},{160,448},{192,480},{... | collective-permute-start | bytes 786440 | tf_op jit(solution)/shard_map/cond/branch_22_fun/ppermute | solution.py:23
  79.0 67.7 %collective-permute-start.174 = (bf16[32,4096]{1,0:T(8,128)(2,1)S(1)}, bf16[32,4096]{1,0:T(8,128)(2,1)S(1)}, u32[]{:S(2)}, u32[]{:S(2)}) collective-permute-start(bf16[32,4096]{1,0:T(8,128)(2,1)S(1)} %get-tuple-element.479), channel_id=1, source_target_pairs={{0,64},{32,96},{64,128},{96,160},{128,192},{160,224},{192,256},{22... | collective-permute-start | bytes 786440 | tf_op jit(solution)/shard_map/ppermute | solution.py:23
  87.5 59.2 %collective-permute-start.175 = (bf16[32,4096]{1,0:T(8,128)(2,1)}, bf16[32,4096]{1,0:T(8,128)(2,1)S(1)}, u32[]{:S(2)}, u32[]{:S(2)}) collective-permute-start(bf16[32,4096]{1,0:T(8,128)(2,1)} %get-tuple-element.481), channel_id=1, source_target_pairs={{0,32},{32,64},{64,96},{96,128},{128,160},{160,192},{192,224},{224... | collective-permute-start | bytes 786440 | tf_op jit(solution)/shard_map/ppermute | solution.py:23

commit v5 on v3

--- a/solution.py
+++ b/solution.py
@@ -14,7 +14,7 @@
 CORES = 2
 ROWS_Y = 4
 VMEM = pl.BlockSpec(memory_space=pltpu.VMEM)
-SMEM = pl.BlockSpec(memory_space=pltpu.SMEM)
+HBM = pl.BlockSpec(memory_space=pltpu.HBM)
 
 
 def shifted(value, axis, steps):
@@ -23,15 +23,16 @@
     return lax.ppermute(value, axis, pairs)
 
 
-def pack_kernel(length_ref, state_ref, gain_ref, message_ref):
+def pack_kernel(length_ref, state_ref, gain_ref, message_ref, wide_ref):
     blocks = state_ref.shape[1] // LANES
     for b in range(blocks):
         message_ref[b] = state_ref[:, b * LANES : (b + 1) * LANES]
     wide = gain_ref[...].astype(jnp.float32)
+    wide_ref[...] = wide
     rows = [wide[:, b * LANES : (b + 1) * LANES] for b in range(blocks)]
     message_ref[blocks] = jnp.concatenate(rows, axis=0).astype(jnp.bfloat16)
-    length = jnp.full(message_ref.shape[1:], length_ref[0], jnp.int32)
-    message_ref[blocks + 1] = length.astype(jnp.float32).astype(jnp.bfloat16)
+    length = length_ref[...].astype(jnp.float32)
+    message_ref[blocks + 1] = jnp.broadcast_to(length, message_ref.shape[1:]).astype(jnp.bfloat16)
 
 
 def packed(states, gain, length):
@@ -39,21 +40,29 @@
     blocks = width // LANES
     return pl.pallas_call(
         pack_kernel,
-        out_shape=jax.ShapeDtypeStruct((blocks + 2, rows, LANES), states.dtype),
-        in_specs=[SMEM, VMEM, VMEM],
-        out_specs=VMEM,
+        out_shape=[
+            jax.ShapeDtypeStruct((blocks + 2, rows, LANES), states.dtype),
+            jax.ShapeDtypeStruct(gain.shape, jnp.float32),
+        ],
+        in_specs=[VMEM] * 3,
+        out_specs=[VMEM] * 2,
         name="pack",
     )(length, states, gain)
 
 
-def steps_kernel(key_len_ref, message_ref, gain_next_ref, memory_ref, *refs):
-    out_refs, (score_ref, state_ref) = refs[:STEPS], refs[STEPS:]
+def steps_kernel(key_len_ref, message_ref, gain_next_ref, held_ref, *refs):
+    out_refs, (score_ref, state_ref, memory_ref, arrival) = refs[:STEPS], refs[STEPS:]
+    fetches = [
+        pltpu.make_async_copy(held_ref.at[half], memory_ref.at[half], arrival.at[half])
+        for half in range(2)
+    ]
+    fetches[0].start()
     rows = message_ref.shape[1]
     width = memory_ref.shape[2]
     heads, keys = width // HD, memory_ref.shape[1]
     blocks = width // LANES
     per_head = HD // LANES
-    key_live = lax.broadcasted_iota(jnp.int32, (rows, keys), 1) < key_len_ref[0]
+    key_live = lax.broadcasted_iota(jnp.int32, (rows, keys), 1) < key_len_ref[...]
     length = message_ref[blocks + 1][:, :1].astype(jnp.float32)
     row_live = lax.broadcasted_iota(jnp.int32, (rows, 1), 0).astype(jnp.float32) < length
     for t in range(STEPS):
@@ -64,6 +73,9 @@
             squares = squares + wide * wide
         mean = jnp.sum(squares, axis=1, keepdims=True) / width
         scale = lax.rsqrt(mean + 1e-06)
+        if t == 0:
+            fetches[0].wait()
+            fetches[1].start()
         for h in range(heads):
             query = jnp.concatenate(
                 [
@@ -79,6 +91,8 @@
                 preferred_element_type=jnp.float32,
             )
             score_ref[h] = jnp.where(key_live, scores * HD ** (-0.5), jnp.float32(-1e30))
+        if t == 0:
+            fetches[1].wait()
         for h in range(heads):
             scores = score_ref[h]
             expo = jnp.exp(scores - jnp.max(scores, axis=1, keepdims=True))
@@ -89,11 +103,12 @@
                 preferred_element_type=jnp.float32,
             ).astype(jnp.bfloat16)
             mixed = jnp.where(row_live, mixed.astype(jnp.float32), 0.0)
-            out_refs[t][:rows, h * HD : (h + 1) * HD] = mixed.astype(jnp.bfloat16)
+            attended_ref = out_refs[t].at[0] if t + 1 == STEPS else out_refs[t]
+            attended_ref[:, h * HD : (h + 1) * HD] = mixed.astype(jnp.bfloat16)
             if t + 1 == STEPS:
                 for j in range(per_head):
                     b = h * per_head + j
-                    out_refs[t][rows:, b * LANES : (b + 1) * LANES] = source[b]
+                    out_refs[t][1, :, b * LANES : (b + 1) * LANES] = source[b]
             else:
                 for j in range(per_head):
                     b = h * per_head + j
@@ -113,23 +128,25 @@
     return pl.pallas_call(
         steps_kernel,
         out_shape=[
-            jax.ShapeDtypeStruct((rows * (1 + (t + 1 == STEPS)), width), jnp.bfloat16)
+            jax.ShapeDtypeStruct((2,) * (t + 1 == STEPS) + (rows, width), jnp.bfloat16)
             for t in range(STEPS)
         ],
-        in_specs=[SMEM, VMEM, VMEM, VMEM],
+        in_specs=[VMEM, VMEM, VMEM, HBM],
         out_specs=[VMEM] * STEPS,
         scratch_shapes=[
             pltpu.VMEM((width // HD, rows, keys), jnp.float32),
             pltpu.VMEM((width // LANES, rows, LANES), jnp.bfloat16),
+            pltpu.VMEM(memory.shape, memory.dtype),
+            pltpu.SemaphoreType.DMA((2,)),
         ],
         compiler_params=pltpu.CompilerParams(vmem_limit_bytes=16 << 20),
         name="steps",
     )(key_len, message, gain_next, memory)
 
 
-def updated(state, gain, attended):
+def updated(state, gain_wide, attended):
     return (
-        state.astype(jnp.float32) + gain.astype(jnp.float32) * attended.astype(jnp.float32)
+        state.astype(jnp.float32) + gain_wide * attended.astype(jnp.float32)
     ).astype(jnp.bfloat16)
 
 
@@ -146,8 +163,18 @@
     return message, shifted(gain, "section", offset - 1)
 
 
-def from_owner(offset, *attended):
-    return tuple(shifted(a, "section", t - offset) for t, a in enumerate(attended))
+def gain_part(cotangent, attended):
+    return sum(
+        jnp.sum(c.astype(jnp.float32) * a.astype(jnp.float32), axis=0, keepdims=True)
+        for c, a in zip(cotangent, attended)
+    )
+
+
+def from_owner(offset, first, middle, last, cotangent, gain_wide):
+    first = shifted(first, "section", -offset)
+    middle = shifted(middle, "section", 1 - offset)
+    last = shifted(last, "section", 2 - offset)
+    return updated(last[1], gain_wide, last[0]), gain_part(cotangent, (first, middle, last[0]))
 
 
 def near_dp_sum(row):
@@ -179,20 +206,13 @@
     state, gain = states[0, 0], section_gain
     offset_index = owner_map[0] - LEAST_OFFSET
 
-    message = packed(state, gain, decode_len[0])
+    message, gain_wide = packed(state, gain, decode_len)
     message, gain_next = by_offset(offset_index, sections, to_owner, message, gain)
-    sent = attended_steps(message, gain_next, memory[0, 0], memory_len[0])
-    sent = by_offset(offset_index, sections, from_owner, *sent)
-
-    rows = state.shape[0]
-    total = jnp.zeros((1, state.shape[1]), jnp.float32)
-    for t in range(STEPS):
-        total = total + jnp.sum(
-            cotangent[0, t, 0].astype(jnp.float32) * sent[t][:rows].astype(jnp.float32),
-            axis=0,
-            keepdims=True,
-        )
-    state = updated(sent[-1][rows:], gain, sent[-1][:rows])
+    held = pltpu.with_memory_space_constraint(memory[0, 0], pltpu.HBM)
+    sent = attended_steps(message, gain_next, held, memory_len)
+    state, total = by_offset(
+        offset_index, sections, from_owner, *sent, cotangent[0, :, 0], gain_wide
+    )
     return (state[None, None], far_dp_sum(near_dp_sum(total)))
 
 

time: 172 us -> 173 us (level)
  the two profiles are of different devices: /device:TPU:2 before, /device:TPU:68 now
where the time goes in v5:
time: 173 us; the launch traced here: 172 us
  waiting for transfers between devices  72.6 us (42%)
  blocking collectives  55.2 us (32%)
  starting transfers between devices  33.8 us (20%)
  Pallas kernels  6.8 us (4%)
  between operations  2.7 us (2%)
    ppermute x5, waiting for transfers between devices, shifted(): return lax.ppermute(value, axis, pairs)  72.6 us
    psum x1, blocking collectives, far_dp_sum(): return lax.psum(row, 'dp', axis_index_groups=groups)  44.8 us
    ppermute x5, starting transfers between devices, shifted(): return lax.ppermute(value, axis, pairs)  33.8 us
    all_to_all x1, blocking collectives, near_dp_sum(): lax.all_to_all(copies, 'dp', 0, 0, axis_index_groups=groups)  10.4 us
    pallas_call x1, Pallas kernels, attended_steps(): pl.pallas_call(steps_kernel, out_shape=[jax.ShapeDtypeStruct((2,) * (t +...  5.77 us
  transfers between devices with their start and end apart: 5, of which 3 were waited for; matrix products, arithmetic and copies ran while one was open for 0% of the time, Pallas kernels for 0%

profile of v5, /device:TPU:68, one launch (start us, length us, event | category | flops | bytes accessed | tf_op | source)
XLA Modules:
  0.0 172.3 jit_solution(9080321166395342142)
XLA Ops:
  0.6 0.0 copy-start
  1.4 1.0 pack.1
  3.7 24.6 %conditional.4 = (bf16[34,32,128]{2,1,0:T(8,128)(2,1)}, bf16[1,4096]{1,0:T(2,128)(2,1)}) conditional(s32[]{:T(128)} %bitcast.261, (bf16[34,32,128]{2,1,0:T(8,128)(2,1)S(1)}, bf16[1,4096]{1,0:T(2,128)(2,1)}) %tuple.358, (bf16[34,32,128]{2,1,0:T(8,128)(2,1)S(1)}, bf16[1,4096]{1,0:T(2,128)(2,1)}) %tuple.358, ...), branch_computations={%region_0.0_spmd, %region_1.0_spmd, %region_2.0_spmd, %region_3.0_... | conditional | bytes 1146976 | solution.py:154
  3.7 7.7 %collective-permute-start.16 = (bf16[34,32,128]{2,1,0:T(8,128)(2,1)S(1)}, bf16[34,32,128]{2,1,0:T(8,128)(2,1)}, u32[]{:S(2)}, u32[]{:S(2)}) collective-permute-start(bf16[34,32,128]{2,1,0:T(8,128)(2,1)S(1)} %get-tuple-element.430), channel_id=1, source_target_pairs={{0,352},{32,384},{64,416},{96,448},{128,480},{160,512},{192,544},{... | collective-permute-start | bytes 835592 | tf_op jit(solution)/shard_map/cond/branch_8_fun/ppermute | solution.py:23
  11.4 7.3 %collective-permute-start.17 = (bf16[1,4096]{1,0:T(2,128)(2,1)}, bf16[1,4096]{1,0:T(2,128)(2,1)}, u32[]{:S(2)}, u32[]{:S(2)}) collective-permute-start(bf16[1,4096]{1,0:T(2,128)(2,1)} %get-tuple-element.431), channel_id=1, source_target_pairs={{0,320},{32,352},{64,384},{96,416},{128,448},{160,480},{192,512},{... | collective-permute-start | bytes 24584 | tf_op jit(solution)/shard_map/cond/branch_8_fun/ppermute | solution.py:23
  18.8 9.5 %collective-permute-done.17 = bf16[1,4096]{1,0:T(2,128)(2,1)} collective-permute-done((bf16[1,4096]{1,0:T(2,128)(2,1)}, bf16[1,4096]{1,0:T(2,128)(2,1)}, u32[]{:S(2)}, u32[]{:S(2)}) %collective-permute-start.17) | collective-permute-done | bytes 8224 | tf_op jit(solution)/shard_map/cond/branch_8_fun/ppermute | solution.py:23
  28.2 0.0 collective-permute-done.16
  28.2 5.8 %steps.1 = (bf16[32,4096]{1,0:T(8,128)(2,1)S(1)}, bf16[32,4096]{1,0:T(8,128)(2,1)S(1)}, bf16[2,32,4096]{2,1,0:T(8,128)(2,1)S(1)}) custom-call(s32[1,1]{1,0:T(1,128)S(6)} %copy.127.key_len_ref, bf16[34,32,128]{2,1,0:T(8,128)(2,1)} %get-tuple-element.629.message_ref, bf16[1,4096]{1,0:T(2,128)(2,1)} %get-tuple-element.630.gain_next_ref, ...), custom_call_target="tpu_custom_call" | custom-call | tf_op jit(solution)/shard_map/steps/pallas_call | solution.py:128
  34.0 0.0 copy-done
  34.0 82.9 %conditional.6 = (f32[1,4096]{1,0:T(1,128)S(1)}, bf16[1,1,32,4096]{3,2,1,0:T(8,128)(2,1)S(1)}) conditional(s32[]{:T(128)} %bitcast.261, (bf16[3,32,4096]{2,1,0:T(8,128)(2,1)S(1)}, bf16[32,4096]{1,0:T(8,128)(2,1)S(1)}, bf16[32,4096]{1,0:T(8,128)(2,1)S(1)}, bf16[2,32,4096]{2,1,0:T(8,128)(2,1)S(1)}, ...), branch_computations={%region_29.0_spmd, %region_33.0_spmd, %region_37.0_spmd, %region_4... | conditional | flops 2224128 | bytes 6684808
  34.1 8.8 %collective-permute-start.84 = (bf16[2,32,4096]{2,1,0:T(8,128)(2,1)S(1)}, bf16[2,32,4096]{2,1,0:T(8,128)(2,1)S(1)}, u32[]{:S(2)}, u32[]{:S(2)}) collective-permute-start(bf16[2,32,4096]{2,1,0:T(8,128)(2,1)S(1)} %get-tuple-element.515), channel_id=1, source_target_pairs={{0,736},{32,768},{64,800},{96,832},{128,864},{160,896},{192,928},{... | collective-permute-start | bytes 1572872 | tf_op jit(solution)/shard_map/cond/branch_8_fun/ppermute | solution.py:23
  42.9 4.6 %collective-permute-start.82 = (bf16[32,4096]{1,0:T(8,128)(2,1)S(1)}, bf16[32,4096]{1,0:T(8,128)(2,1)S(1)}, u32[]{:S(2)}, u32[]{:S(2)}) collective-permute-start(bf16[32,4096]{1,0:T(8,128)(2,1)S(1)} %get-tuple-element.513), channel_id=1, source_target_pairs={{0,672},{32,704},{64,736},{96,768},{128,800},{160,832},{192,864},{... | collective-permute-start | bytes 786440 | tf_op jit(solution)/shard_map/cond/branch_8_fun/ppermute | solution.py:23
  47.4 5.4 %collective-permute-start.83 = (bf16[32,4096]{1,0:T(8,128)(2,1)S(1)}, bf16[32,4096]{1,0:T(8,128)(2,1)S(1)}, u32[]{:S(2)}, u32[]{:S(2)}) collective-permute-start(bf16[32,4096]{1,0:T(8,128)(2,1)S(1)} %get-tuple-element.514), channel_id=1, source_target_pairs={{0,704},{32,736},{64,768},{96,800},{128,832},{160,864},{192,896},{... | collective-permute-start | bytes 786440 | tf_op jit(solution)/shard_map/cond/branch_8_fun/ppermute | solution.py:23
  52.9 42.6 %collective-permute-done.82 = bf16[32,4096]{1,0:T(8,128)(2,1)S(1)} collective-permute-done((bf16[32,4096]{1,0:T(8,128)(2,1)S(1)}, bf16[32,4096]{1,0:T(8,128)(2,1)S(1)}, u32[]{:S(2)}, u32[]{:S(2)}) %collective-permute-start.82) | collective-permute-done | bytes 262176 | tf_op jit(solution)/shard_map/cond/branch_8_fun/ppermute | solution.py:23
  95.5 20.6 %collective-permute-done.83 = bf16[32,4096]{1,0:T(8,128)(2,1)S(1)} collective-permute-done((bf16[32,4096]{1,0:T(8,128)(2,1)S(1)}, bf16[32,4096]{1,0:T(8,128)(2,1)S(1)}, u32[]{:S(2)}, u32[]{:S(2)}) %collective-permute-start.83) | collective-permute-done | bytes 262176 | tf_op jit(solution)/shard_map/cond/branch_8_fun/ppermute | solution.py:23
  116.1 0.2 fusion.43
  116.3 0.0 collective-permute-done.84
  116.3 0.1 fusion.40
  116.4 0.1 fusion.42
  116.9 0.0 copy-start.1
  116.9 0.1 broadcast_in_dim.66
  117.0 10.4 %all_to_all.6 = f32[8,1,4096]{2,1,0:T(1,128)S(1)} all-to-all(f32[8,1,4096]{2,1,0:T(1,128)S(1)} %broadcast_in_dim.66), channel_id=1, replica_groups={{0,1,8,9,16,17,24,25},{2,3,10,11,18,19,26,27},{4,5,12,13,20,21,28,29},{..., dimensions={0} | all-to-all | bytes 262144 | tf_op jit(solution)/shard_map/all_to_all | solution.py:189
  127.4 0.1 reduce_sum.792
  127.5 44.8 %psum.7 = f32[1,4096]{1,0:T(1,128)} all-reduce(f32[1,4096]{1,0:T(1,128)S(1)} %bitcast.618), channel_id=1, replica_groups={{0,2,4,6},{1,3,5,7},{8,10,12,14},{9,11,13,15},{16,18,20,22},{17,19,21,2..., use_global_device_ids=true, to_apply=%region_146.0 | all-reduce | flops 4096 | bytes 32768 | tf_op jit(solution)/shard_map/psum | solution.py:201
  172.3 0.0 copy-done.1
  (1 shorter events, 0.0 us)
Async XLA Ops:
  0.6 33.4 %copy-start = (bf16[1,3,1,32,4096]{4,3,2,1,0:T(8,128)(2,1)S(1)}, bf16[1,3,1,32,4096]{4,3,2,1,0:T(8,128)(2,1)}, u32[]{:S(2)}) copy-start(bf16[1,3,1,32,4096]{4,3,2,1,0:T(8,128)(2,1)} %param.71) | copy-start | bytes 2359300
  3.7 24.5 %collective-permute-start.16 = (bf16[34,32,128]{2,1,0:T(8,128)(2,1)S(1)}, bf16[34,32,128]{2,1,0:T(8,128)(2,1)}, u32[]{:S(2)}, u32[]{:S(2)}) collective-permute-start(bf16[34,32,128]{2,1,0:T(8,128)(2,1)S(1)} %get-tuple-element.430), channel_id=1, source_target_pairs={{0,352},{32,384},{64,416},{96,448},{128,480},{160,512},{192,544},{... | collective-permute-start | bytes 835592 | tf_op jit(solution)/shard_map/cond/branch_8_fun/ppermute | solution.py:23
  11.4 16.8 %collective-permute-start.17 = (bf16[1,4096]{1,0:T(2,128)(2,1)}, bf16[1,4096]{1,0:T(2,128)(2,1)}, u32[]{:S(2)}, u32[]{:S(2)}) collective-permute-start(bf16[1,4096]{1,0:T(2,128)(2,1)} %get-tuple-element.431), channel_id=1, source_target_pairs={{0,320},{32,352},{64,384},{96,416},{128,448},{160,480},{192,512},{... | collective-permute-start | bytes 24584 | tf_op jit(solution)/shard_map/cond/branch_8_fun/ppermute | solution.py:23
  34.1 82.2 %collective-permute-start.84 = (bf16[2,32,4096]{2,1,0:T(8,128)(2,1)S(1)}, bf16[2,32,4096]{2,1,0:T(8,128)(2,1)S(1)}, u32[]{:S(2)}, u32[]{:S(2)}) collective-permute-start(bf16[2,32,4096]{2,1,0:T(8,128)(2,1)S(1)} %get-tuple-element.515), channel_id=1, source_target_pairs={{0,736},{32,768},{64,800},{96,832},{128,864},{160,896},{192,928},{... | collective-permute-start | bytes 1572872 | tf_op jit(solution)/shard_map/cond/branch_8_fun/ppermute | solution.py:23
  42.9 52.6 %collective-permute-start.82 = (bf16[32,4096]{1,0:T(8,128)(2,1)S(1)}, bf16[32,4096]{1,0:T(8,128)(2,1)S(1)}, u32[]{:S(2)}, u32[]{:S(2)}) collective-permute-start(bf16[32,4096]{1,0:T(8,128)(2,1)S(1)} %get-tuple-element.513), channel_id=1, source_target_pairs={{0,672},{32,704},{64,736},{96,768},{128,800},{160,832},{192,864},{... | collective-permute-start | bytes 786440 | tf_op jit(solution)/shard_map/cond/branch_8_fun/ppermute | solution.py:23
  47.4 68.6 %collective-permute-start.83 = (bf16[32,4096]{1,0:T(8,128)(2,1)S(1)}, bf16[32,4096]{1,0:T(8,128)(2,1)S(1)}, u32[]{:S(2)}, u32[]{:S(2)}) collective-permute-start(bf16[32,4096]{1,0:T(8,128)(2,1)S(1)} %get-tuple-element.514), channel_id=1, source_target_pairs={{0,704},{32,736},{64,768},{96,800},{128,832},{160,864},{192,896},{... | collective-permute-start | bytes 786440 | tf_op jit(solution)/shard_map/cond/branch_8_fun/ppermute | solution.py:23
  116.9 55.4 %copy-start.1 = (bf16[1,1,32,4096]{3,2,1,0:T(8,128)(2,1)}, bf16[1,1,32,4096]{3,2,1,0:T(8,128)(2,1)S(1)}, u32[]{:S(2)}) copy-start(bf16[1,1,32,4096]{3,2,1,0:T(8,128)(2,1)S(1)} %get-tuple-element.640) | copy-start | bytes 786436
